TPU v7x, 256 devices: a whole 4x4x8 slice. The times are simulated.
256 devices in a mesh: replica: 16 (over x, y_hi, core), tensor: 16 (over z, y_lo).
Axes of the slice: x: 4, y: 4 (y_hi: 2, y_lo: 2; y = y_hi * 2 + y_lo), z: 8, core: 2. Of those that a mesh axis runs over, the one named last changes fastest.
Arguments:
- inputs: bfloat16 [32768, 4096], P('replica', 'tensor'), may hold values from -6 to 6
- out_grad: bfloat16 [32768, 2560], P(('replica', 'tensor')), may hold values from -6 to 6
- weight: bfloat16 [4096, 2560], P('tensor'), may hold values from -0.09375 to 0.09375
- momentum: bfloat16 [16, 4096, 2560], P('replica', 'tensor'), may hold values from -6 to 6
- selected: int32 [2560, 64], P('tensor'), may hold values from 0 to 4095, as said below
Outputs:
- input_grad: bfloat16 [32768, 4096], P('replica', 'tensor')
- new_momentum: bfloat16 [16, 4096, 2560], P('replica', 'tensor')
- update: bfloat16 [4096, 2560], P('tensor')
Inputs may be any that keep to these rules, and one draw needn't show every extreme that they name: `selected`: each row holds 64 different frequency numbers u * 64 + v of one block; the same selection holds for every replica.
All inputs are finite; a program needn't handle non-finite values.
Results may differ from a plain program's by a relative error of at most 0.001.
Values may be sent and summed in bfloat16 or wider, within the bound.
No kernel may reach another device: no remote copies, remote signals or barrier semaphores. Data moves between devices by JAX's collectives and lax.ppermute only.
A program may use at most 128 MiB of HBM per device.

v0:
```python
import math

import jax
import jax.numpy as jnp
import numpy as np
from jax import lax
from jax.experimental import pallas as pl
from jax.experimental.pallas import tpu as pltpu
from jax.sharding import Mesh
from jax.sharding import PartitionSpec as P


BLK = 64
TOPK = 64
TENSOR = ("z", "yl")
REPLICA = ("x", "yh", "core")

CUT = 1152
A4 = 640
B4 = 640
OFFSETS = (0, 1, -1, 2, -2, 3, -3, 4)


def dct_table():
    k = np.arange(BLK)
    table = np.cos(np.pi * np.outer(k, 2 * k + 1) / (2 * BLK)) * math.sqrt(2.0 / BLK)
    table[0] = math.sqrt(1.0 / BLK)
    return table.astype(np.float32)


def bf16_parts(table, n):
    parts, rest = [], table.astype(np.float32)
    for _ in range(n):
        part = rest.astype(jnp.bfloat16)
        parts.append(part)
        rest = rest - part.astype(np.float32)
    return parts


def dot(a, b, dims=((1,), (0,))):
    return lax.dot_general(a, b, (dims, ((), ())), preferred_element_type=jnp.float32)


def split(x):
    hi = x.astype(jnp.bfloat16)
    lo = (x - hi.astype(jnp.float32)).astype(jnp.bfloat16)
    return hi, lo


def vmem(n):
    return [pl.BlockSpec(memory_space=pltpu.VMEM)] * n


SMEM = pl.BlockSpec(memory_space=pltpu.SMEM)


def call(kernel, out, ins, specs):
    many = isinstance(out, (list, tuple))
    return pl.pallas_call(
        kernel,
        out_shape=out,
        in_specs=specs,
        out_specs=vmem(len(out)) if many else vmem(1)[0],
        cost_estimate=pl.CostEstimate(flops=10**9, bytes_accessed=0, transcendentals=0),
        compiler_params=pltpu.CompilerParams(vmem_limit_bytes=8 * 2**20),
    )(*ins)


def shape(s, d):
    return jax.ShapeDtypeStruct(s, d)


def prep_operands(idx, inputs, weight):
    tokens, rows = inputs.shape
    cols = weight.shape[1]

    def kernel(idx_ref, x_ref, w_ref, xt_ref, wt_ref):
        for s in range(tokens // 128):
            at = pl.multiple_of(idx_ref[s] * 128, 128)
            xt_ref[:, s * 128:(s + 1) * 128] = x_ref[pl.ds(at, 128), :].T
        for c in range(cols // 256):
            wt_ref[c * 256:(c + 1) * 256, :] = w_ref[:, c * 256:(c + 1) * 256].T

    return call(
        kernel,
        [shape((rows, tokens), jnp.bfloat16), shape((cols, rows), jnp.bfloat16)],
        (idx, inputs, weight),
        [SMEM] + vmem(2),
    )


def prep_bases(selected, brows):
    blocks = selected.shape[0]
    per = blocks // 2 // brows
    table = dct_table()
    eye = np.eye(2, dtype=np.float32)
    tt = jnp.asarray(np.concatenate(bf16_parts(table.T, 3), axis=1))
    t2 = jnp.asarray(np.concatenate(bf16_parts(table.T, 2), axis=0))
    g2 = jnp.asarray(
        np.concatenate([np.kron(eye, p.astype(np.float32)).astype(jnp.bfloat16) for p in bf16_parts(table, 2)], axis=1)
    )

    def kernel(sel_ref, tt_ref, t2_ref, g2_ref, *outs):
        lane = lax.broadcasted_iota(jnp.int32, (1, 128), 1)
        base = jnp.where(lane >= BLK, BLK, 0)
        row64 = lax.broadcasted_iota(jnp.int32, (BLK, 128), 0)
        row128 = lax.broadcasted_iota(jnp.int32, (128, 128), 0)

        def one(r, cp):
            rt, ct, cd = outs[r], outs[brows + r], outs[2 * brows + r]
            at = (r * per + cp) * 2
            sel = jnp.concatenate([sel_ref[pl.ds(at, 1), :], sel_ref[pl.ds(at + 1, 1), :]], axis=1)
            u = sel >> 6
            v = sel & 63
            ohu = jnp.where(row64 == u, 1.0, 0.0).astype(jnp.bfloat16)
            ohv = jnp.where(row64 == v, 1.0, 0.0).astype(jnp.bfloat16)
            wide = jnp.where(row128 == v + base, 1.0, 0.0).astype(jnp.bfloat16)
            rt[cp] = dot(tt_ref[...], jnp.concatenate([ohu, ohu, ohu], axis=0))
            both = dot(t2_ref[...], ohv).astype(jnp.bfloat16)
            ct[cp, :, :128] = both[:BLK]
            ct[cp, :, 128:] = both[BLK:]
            full = dot(wide, g2_ref[...], ((0,), (0,)))
            cd[cp] = (full[:BLK] + full[BLK:]).astype(jnp.bfloat16)

        def group(g, _):
            for i in range(5):
                for r in range(brows):
                    one(r, g * 5 + i)
            return 0

        lax.fori_loop(0, per // 5, group, 0)

    f32 = [shape((per, BLK, 128), jnp.float32)] * brows
    b16 = [shape((per, BLK, 256), jnp.bfloat16)] * brows
    outs = call(kernel, f32 + b16 + b16, (selected, tt, t2, g2), vmem(4))
    return outs[:brows], outs[brows:2 * brows], outs[2 * brows:]


def product(x, pair):
    n = x.shape[0]
    lane = lax.broadcasted_iota(jnp.int32, (BLK, 256), 1)
    first = (lane & BLK) == 0
    none = jnp.zeros_like(pair)
    full = jnp.concatenate([jnp.where(first, pair, none), jnp.where(first, none, pair)], axis=0)
    y = dot(jnp.concatenate(split(x), axis=0), full)
    return (y[:n, :128] + y[n:, :128]) + (y[:n, 128:] + y[n:, 128:])


def over_pairs(brows, pcols, run):
    def group(g, _):
        for i in range(5):
            cp = g * 5 + i
            at = pl.ds(pl.multiple_of(cp * 128, 128), 128)
            for r in range(brows):
                run(r, cp, r * pcols + cp, slice(r * BLK, (r + 1) * BLK), at)
        return 0

    lax.fori_loop(0, pcols // 5, group, 0)


def distinct(pieces):
    arrays = list({id(p[0]): p[0] for p in pieces}.values())
    where = {id(x): i for i, x in enumerate(arrays)}
    return arrays, [(where[id(p[0])], *p[1:]) for p in pieces]


def view(refs, which, sub):
    return refs[which][...] if sub is None else refs[which][sub]


def wgrad_into(acc_ref, start, xt_ref, pieces, refs, scale):
    edges = sorted({p[4] for p in pieces} | {p[4] + p[5] for p in pieces} | {0, acc_ref.shape[1]})
    for lo, hi in zip(edges[:-1], edges[1:]):
        for at in range(lo, hi, 256):
            width = min(256, hi - at)
            total = None
            for which, sub, slot, slots, c, n in pieces:
                if not (c <= at and at + width <= c + n):
                    continue
                cut = slice(at - c, at - c + width)
                g = refs[which][..., cut] if sub is None else refs[which][sub, :, cut]
                part = dot(xt_ref[:, slot * 128:(slot + slots) * 128], g.reshape(slots * 128, width))
                total = part if total is None else total + part
            first = start(at, width)
            acc_ref[:, at:at + width] = first if total is None else first + total * scale


def wgrad_first(xt, momentum, pieces, scale):
    rows, cols = momentum.shape
    arrays, pieces = distinct(pieces)

    def kernel(xt_ref, m_ref, *refs):
        wgrad_into(
            refs[-1],
            lambda at, n: 0.999 * m_ref[:, at:at + n].astype(jnp.float32),
            xt_ref, pieces, refs[:-1], scale,
        )

    return call(kernel, shape((rows, cols), jnp.float32), (xt, momentum, *arrays), vmem(2 + len(arrays)))


def wgrad_more(xt, acc, pieces, scale):
    arrays, pieces = distinct(pieces)

    def kernel(xt_ref, in_ref, *refs):
        wgrad_into(refs[-1], lambda at, n: in_ref[:, at:at + n], xt_ref, pieces, refs[:-1], scale)

    return call(kernel, shape(acc.shape, jnp.float32), (xt, acc, *arrays), vmem(2 + len(arrays)))


def split_columns(g):
    n, cols = g.shape

    def kernel(g_ref, a_ref, b_ref):
        a_ref[...] = g_ref[:, :CUT]
        b_ref[...] = g_ref[:, CUT:]

    outs = [shape((n, CUT), g.dtype), shape((n, cols - CUT), g.dtype)]
    return call(kernel, outs, (g,), vmem(1))


def stacked(a, b):
    def kernel(a_ref, b_ref, out_ref):
        out_ref[0] = a_ref[...]
        out_ref[1] = b_ref[...]

    return call(kernel, shape((2, *a.shape), a.dtype), (a, b), vmem(2))


def beside(a, b):
    m = a.shape[1]

    def kernel(a_ref, b_ref, out_ref):
        out_ref[:, :m] = a_ref[...]
        out_ref[:, m:] = b_ref[...]

    return call(kernel, shape((a.shape[0], m + b.shape[1]), a.dtype), (a, b), vmem(2))


def wgrad_encode(xt, acc, pieces, rts, cts, scale):
    arrays, pieces = distinct(pieces)
    rows, cols = acc.shape
    brows = rows // BLK
    pcols = cols // 128

    def kernel(xt_ref, in_ref, *refs):
        rt, ct = refs[:brows], refs[brows:2 * brows]
        *ins, acc_ref, sent_ref = refs[2 * brows:]
        wgrad_into(acc_ref, lambda at, n: in_ref[:, at:at + n], xt_ref, pieces, ins, scale)

        def one(r, cp, p, at, cols_at):
            u = product(acc_ref[at, cols_at], ct[r][cp])
            sent_ref[pl.ds(p, 1), :] = jnp.sum(u * rt[r][cp], axis=0, keepdims=True)

        over_pairs(brows, pcols, one)

    return call(
        kernel,
        [shape(acc.shape, jnp.float32), shape((brows * pcols, 128), jnp.float32)],
        (xt, acc, *rts, *cts, *arrays),
        vmem(2 + 2 * brows + len(arrays)),
    )


def residual(acc, sent, rts, cds):
    rows, cols = acc.shape
    pcols = cols // 128
    brows = rows // BLK

    def kernel(acc_ref, sent_ref, *refs):
        rt, cd, out_ref = refs[:brows], refs[brows:2 * brows], refs[-1]

        def one(r, cp, p, at, cols_at):
            e = product(rt[r][cp] * sent_ref[pl.ds(p, 1), :], cd[r][cp])
            out_ref[at, cols_at] = (acc_ref[at, cols_at] - e).astype(jnp.bfloat16)

        over_pairs(brows, pcols, one)

    return call(kernel, shape(acc.shape, jnp.bfloat16), (acc, sent, *rts, *cds), vmem(2 + 2 * brows))


def decode_update(total, rts, cds, rows, cols, factor):
    pcols = cols // 128
    brows = rows // BLK

    def kernel(s_ref, *refs):
        rt, cd, out_ref = refs[:brows], refs[brows:2 * brows], refs[-1]

        def one(r, cp, p, at, cols_at):
            e = product(rt[r][cp] * (s_ref[pl.ds(p, 1), :] * factor), cd[r][cp])
            out_ref[at, cols_at] = e.astype(jnp.bfloat16)

        over_pairs(brows, pcols, one)

    return call(kernel, shape((rows, cols), jnp.bfloat16), (total, *rts, *cds), vmem(1 + 2 * brows))


def input_grad(idx, wt, pieces, tokens, before):
    rows = wt.shape[1]
    given = [] if before is None else [before]
    arrays, pieces = distinct(pieces)

    def kernel(idx_ref, wt_ref, *refs):
        out_ref = refs[-1]
        if given:
            out_ref[...] = refs[-2][...]
        for s in sorted({p[2] for p in pieces}):
            total = None
            for which, sub, slot, c, n in pieces:
                if slot == s:
                    part = dot(view(refs, which, sub), wt_ref[c:c + n, :])
                    total = part if total is None else total + part
            at = pl.multiple_of(idx_ref[s] * 128, 128)
            out_ref[pl.ds(at, 128), :] = total.astype(jnp.bfloat16)

    return call(
        kernel,
        shape((tokens, rows), jnp.bfloat16),
        (idx, wt, *arrays, *given),
        [SMEM] + vmem(1 + len(arrays) + len(given)),
    )


def zp(x, step):
    n = lax.axis_size("z")
    return lax.ppermute(x, "z", [(i, (i + step) % n) for i in range(n)])


def yp(x):
    return lax.ppermute(x, "yl", [(0, 1), (1, 0)])


def over_replicas(s):
    def shift(v, axis, step):
        n = lax.axis_size(axis)
        return lax.ppermute(v, axis, [(i, (i + step) % n) for i in range(n)])

    a = shift(s, "yh", 1)
    b = lax.ppermute(s, ("yh", "core"), [(i, i ^ 3) for i in range(4)])
    c = shift(s, "core", 1)
    s = (s + c) + (a + b)
    e = shift(s, "x", 2)
    f = shift(s, "x", 1)
    g = shift(s, "x", -1)
    return (s + e) + (f + g)


def step(inputs, out_grad, weight, momentum, selected):
    rows, cols = weight.shape
    scale = 1.0 / math.sqrt(inputs.shape[0])
    z, yl = lax.axis_index("z"), lax.axis_index("yl")
    nz = lax.axis_size("z")
    idx = jnp.stack([((z - d) % nz) * 2 + (yl + dy) % 2 for d in OFFSETS for dy in range(2)]).astype(jnp.int32)

    a, b = split_columns(out_grad)
    xt, wt = prep_operands(idx, inputs, weight)
    rts, cts, cds = prep_bases(selected, rows // BLK)

    def ring(x, cut):
        got = {0: x}
        up = dn = x
        for d in (1, 2, 3):
            up, dn = zp(up, 1), zp(dn, -1)
            got[d], got[-d] = up, dn
        got[4] = zp(up[..., :cut], 1), zp(dn[..., cut:], -1)
        return got

    ra = ring(stacked(a, yp(a)), A4)
    rb = ring(b, B4)
    own = {0: b, 4: beside(*rb[4])}
    own.update({d: stacked(rb[d], rb[-d]) for d in (1, 2, 3)})
    other = {d: yp(own[d]) for d in range(5)}

    def part_a(d):
        if d != 4:
            return [(ra[d], None, 0, CUT)]
        return [(ra[4][0], None, 0, A4), (ra[4][1], None, A4, CUT - A4)]

    def part_b(store, d):
        return store[abs(d)], (None if d in (0, 4) else int(d < 0)), CUT, cols - CUT

    def slot(d):
        return 2 * OFFSETS.index(d)

    def w_pieces(stage):
        pieces = []
        for kind, *offsets in stage:
            for d in offsets:
                if kind == "a":
                    pieces += [(x, sub, slot(d), 2, c, n) for x, sub, c, n in part_a(d)]
                else:
                    x, sub, c, n = part_b(own if kind == "own" else other, d)
                    pieces.append((x, sub, slot(d) + (kind == "other"), 1, c, n))
        return pieces

    acc = wgrad_first(xt, momentum[0], w_pieces([("own", 0, 1, -1), ("other", 0), ("a", 0, 1, -1)]), scale)
    acc = wgrad_more(xt, acc, w_pieces([("own", 2, -2, 3, -3), ("other", 1, -1, 2, -2), ("a", 2, -2)]), scale)
    acc = wgrad_more(xt, acc, w_pieces([("own", 4), ("a", 3, -3)]), scale)
    acc, sent = wgrad_encode(xt, acc, w_pieces([("other", 3, -3, 4), ("a", 4)]), rts, cts, scale)
    total = over_replicas(sent)

    def g_pieces(offsets):
        pieces = []
        for d in offsets:
            for dy, store in enumerate((own, other)):
                x, sub, c, n = part_b(store, d)
                pieces.append((x, sub, slot(d) + dy, c, n))
                pieces += [(x, dy, slot(d) + dy, c, n) for x, sub, c, n in part_a(d)]
        return pieces

    dacts = None
    for offsets in ((0, 1, -1), (2, -2), (3, -3), (4,)):
        dacts = input_grad(idx, wt, g_pieces(offsets), inputs.shape[0], dacts)
    fresh = residual(acc, sent, rts, cds)
    factor = BLK / math.sqrt(TOPK) / math.prod(lax.axis_size(a) for a in REPLICA)
    update = decode_update(total, rts, cds, rows, cols, factor)
    return dacts, fresh[None], update


def solution(mesh):
    finer = Mesh(mesh.devices.reshape(4, 2, 2, 8, 2), REPLICA + TENSOR)
    whole = REPLICA + TENSOR
    in_specs = (P(REPLICA, TENSOR), P(whole, None), P(TENSOR, None), P(REPLICA, TENSOR, None), P(TENSOR, None))
    out_specs = (P(REPLICA, TENSOR), P(REPLICA, TENSOR, None), P(TENSOR, None))
    return jax.shard_map(step, mesh=finer, in_specs=in_specs, out_specs=out_specs, check_vma=False)
```

profile of v0, /device:TPU:1, one launch (start us, length us, event | category | flops | bytes accessed | tf_op | source)
XLA Modules:
  0.0 125.8 jit_solution(13697718098298048986)
XLA Ops:
  0.6 1.1 copy-done.14
  1.8 2.2 %collective-permute-start.8 = (bf16[128,1152]{1,0:T(8,128)(2,1)S(1)}, bf16[128,1152]{1,0:T(8,128)(2,1)S(1)}, u32[]{:S(2)}, u32[]{:S(2)}) collective-permute-start(bf16[128,1152]{1,0:T(8,128)(2,1)S(1)} %get-tuple-element.23.a_ref), channel_id=1, source_target_pairs={{0,1},{1,0},{2,3},{3,2},{4,5},{5,4},{6,7},{7,6},{8,9},{9,8},{10,11... | collective-permute-start | bytes 884744 | tf_op jit(solution)/shard_map/ppermute | solution.py:330
  4.0 1.6 %collective-permute-start = (bf16[128,1408]{1,0:T(8,128)(2,1)S(1)}, bf16[128,1408]{1,0:T(8,128)(2,1)S(1)}, u32[]{:S(2)}, u32[]{:S(2)}) collective-permute-start(bf16[128,1408]{1,0:T(8,128)(2,1)S(1)} %get-tuple-element.22.refs_0_), channel_id=1, source_target_pairs={{0,2},{2,4},{4,6},{6,8},{8,10},{10,12},{12,14},{14,0},{1,3},{3,5},... | collective-permute-start | bytes 1081352 | tf_op jit(solution)/shard_map/ppermute | solution.py:326
  5.6 3.9 %collective-permute-done.8.b_ref = bf16[128,1152]{1,0:T(8,128)(2,1)S(1)} collective-permute-done((bf16[128,1152]{1,0:T(8,128)(2,1)S(1)}, bf16[128,1152]{1,0:T(8,128)(2,1)S(1)}, u32[]{:S(2)}, u32[]{:S(2)}) %collective-permute-start.8) | collective-permute-done | bytes 294944 | tf_op jit(solution)/shard_map/ppermute | solution.py:330
  9.6 0.0 copy-start
  9.6 2.8 %collective-permute-start.9 = (bf16[2,128,1152]{2,1,0:T(8,128)(2,1)S(1)}, bf16[2,128,1152]{2,1,0:T(8,128)(2,1)S(1)}, u32[]{:S(2)}, u32[]{:S(2)}) collective-permute-start(bf16[2,128,1152]{2,1,0:T(8,128)(2,1)S(1)} %shard_map.106.refs_1_.refs_3_), channel_id=1, source_target_pairs={{0,2},{2,4},{4,6},{6,8},{8,10},{10,12},{12,14},{14,0},{1,3},{3,5},... | collective-permute-start | bytes 1769480 | tf_op jit(solution)/shard_map/ppermute | solution.py:326
  12.4 4.0 %collective-permute-start.13 = (bf16[2,128,1152]{2,1,0:T(8,128)(2,1)S(1)}, bf16[2,128,1152]{2,1,0:T(8,128)(2,1)}, u32[]{:S(2)}, u32[]{:S(2)}) collective-permute-start(bf16[2,128,1152]{2,1,0:T(8,128)(2,1)S(1)} %shard_map.106.refs_1_.refs_3_), channel_id=1, source_target_pairs={{0,14},{2,0},{4,2},{6,4},{8,6},{10,8},{12,10},{14,12},{1,15},{3,1}... | collective-permute-start | bytes 1769480 | tf_op jit(solution)/shard_map/ppermute | solution.py:326
  16.4 1.4 %collective-permute-start.4 = (bf16[128,1408]{1,0:T(8,128)(2,1)S(1)}, bf16[128,1408]{1,0:T(8,128)(2,1)S(1)}, u32[]{:S(2)}, u32[]{:S(2)}) collective-permute-start(bf16[128,1408]{1,0:T(8,128)(2,1)S(1)} %get-tuple-element.22.refs_0_), channel_id=1, source_target_pairs={{0,14},{2,0},{4,2},{6,4},{8,6},{10,8},{12,10},{14,12},{1,15},{3,1}... | collective-permute-start | bytes 1081352 | tf_op jit(solution)/shard_map/ppermute | solution.py:326
  17.8 1.3 %collective-permute-start.20 = (bf16[128,1408]{1,0:T(8,128)(2,1)S(1)}, bf16[128,1408]{1,0:T(8,128)(2,1)S(1)}, u32[]{:S(2)}, u32[]{:S(2)}) collective-permute-start(bf16[128,1408]{1,0:T(8,128)(2,1)S(1)} %get-tuple-element.22.refs_0_), channel_id=1, source_target_pairs={{0,1},{1,0},{2,3},{3,2},{4,5},{5,4},{6,7},{7,6},{8,9},{9,8},{10,11... | collective-permute-start | bytes 1081352 | tf_op jit(solution)/shard_map/ppermute | solution.py:330
  19.1 0.0 collective-permute-done.a_ref
  19.1 0.1 collective-permute-start.1
  19.1 16.1 %collective-permute-done.4.b_ref = bf16[128,1408]{1,0:T(8,128)(2,1)S(1)} collective-permute-done((bf16[128,1408]{1,0:T(8,128)(2,1)S(1)}, bf16[128,1408]{1,0:T(8,128)(2,1)S(1)}, u32[]{:S(2)}, u32[]{:S(2)}) %collective-permute-start.4) | collective-permute-done | bytes 360480 | tf_op jit(solution)/shard_map/ppermute | solution.py:326
  35.3 3.4 %collective-permute-start.5 = (bf16[128,1408]{1,0:T(8,128)(2,1)S(1)}, bf16[128,1408]{1,0:T(8,128)(2,1)}, u32[]{:S(2)}, u32[]{:S(2)}) collective-permute-start(bf16[128,1408]{1,0:T(8,128)(2,1)S(1)} %collective-permute-done.4.b_ref), channel_id=1, source_target_pairs={{0,14},{2,0},{4,2},{6,4},{8,6},{10,8},{12,10},{14,12},{1,15},{3,1}... | collective-permute-start | bytes 1081352 | tf_op jit(solution)/shard_map/ppermute | solution.py:326
  38.7 0.1 shard_map.109.refs_3_.refs_1_
  38.7 0.0 collective-permute-done.20.refs_2_
  38.8 1.4 %collective-permute-start.21 = (bf16[2,128,1408]{2,1,0:T(8,128)(2,1)S(1)}, bf16[2,128,1408]{2,1,0:T(8,128)(2,1)S(1)}, u32[]{:S(2)}, u32[]{:S(2)}) collective-permute-start(bf16[2,128,1408]{2,1,0:T(8,128)(2,1)S(1)} %shard_map.109.refs_3_.refs_1_), channel_id=1, source_target_pairs={{0,1},{1,0},{2,3},{3,2},{4,5},{5,4},{6,7},{7,6},{8,9},{9,8},{10,11... | collective-permute-start | bytes 2162696 | tf_op jit(solution)/shard_map/ppermute | solution.py:330
  40.2 0.0 collective-permute-done.13.refs_6_.refs_5_
  40.2 2.7 %collective-permute-start.14 = (bf16[2,128,1152]{2,1,0:T(8,128)(2,1)}, bf16[2,128,1152]{2,1,0:T(8,128)(2,1)}, u32[]{:S(2)}, u32[]{:S(2)}) collective-permute-start(bf16[2,128,1152]{2,1,0:T(8,128)(2,1)} %collective-permute-done.13.refs_6_.refs_5_), channel_id=1, source_target_pairs={{0,14},{2,0},{4,2},{6,4},{8,6},{10,8},{12,10},{14,12},{1,15},{3,1}... | collective-permute-start | bytes 1769480 | tf_op jit(solution)/shard_map/ppermute | solution.py:326
  42.8 1.2 collective-permute-done.5.b_ref
  44.1 3.5 %collective-permute-start.6 = (bf16[128,1408]{1,0:T(8,128)(2,1)}, bf16[128,1408]{1,0:T(8,128)(2,1)}, u32[]{:S(2)}, u32[]{:S(2)}) collective-permute-start(bf16[128,1408]{1,0:T(8,128)(2,1)} %collective-permute-done.5.b_ref), channel_id=1, source_target_pairs={{0,14},{2,0},{4,2},{6,4},{8,6},{10,8},{12,10},{14,12},{1,15},{3,1}... | collective-permute-start | bytes 1081352 | tf_op jit(solution)/shard_map/ppermute | solution.py:326
  47.6 1.1 shard_map.108.refs_0_
  48.7 12.4 %collective-permute-done.2.a_ref = bf16[128,1408]{1,0:T(8,128)(2,1)S(1)} collective-permute-done((bf16[128,1408]{1,0:T(8,128)(2,1)S(1)}, bf16[128,1408]{1,0:T(8,128)(2,1)S(1)}, u32[]{:S(2)}, u32[]{:S(2)}) %collective-permute-start.2) | collective-permute-done | bytes 360480 | tf_op jit(solution)/shard_map/ppermute | solution.py:326
  61.0 0.2 collective-permute-start.19
  61.2 0.0 collective-permute-done.10.refs_1_.refs_4_
  61.2 0.6 copy-done.9
  61.8 0.9 copy.11.sel_ref
  62.7 0.7 stack.67.idx_ref
  63.4 0.9 slice.16
  64.3 0.2 collective-permute-done.6.b_ref
  64.5 0.4 collective-permute-start.3
  65.0 3.0 %collective-permute-start.15 = (bf16[2,128,1152]{2,1,0:T(8,128)(2,1)}, bf16[2,128,1152]{2,1,0:T(8,128)(2,1)S(1)}, u32[]{:S(2)}, u32[]{:S(2)}) collective-permute-start(bf16[2,128,1152]{2,1,0:T(8,128)(2,1)} %collective-permute-done.14.refs_3_.refs_5_), channel_id=1, source_target_pairs={{0,14},{2,0},{4,2},{6,4},{8,6},{10,8},{12,10},{14,12},{1,15},{3,1}... | collective-permute-start | bytes 1769480 | tf_op jit(solution)/shard_map/ppermute | solution.py:326
  67.9 1.0 copy-done.10
  68.9 1.2 shard_map.107.refs_0_.refs_1_
  70.1 0.0 copy-start.15
  70.1 0.0 copy-start.16
  70.1 0.0 copy-start.17
  70.2 1.4 %collective-permute-start.18 = (bf16[2,128,1408]{2,1,0:T(8,128)(2,1)S(1)}, bf16[2,128,1408]{2,1,0:T(8,128)(2,1)S(1)}, u32[]{:S(2)}, u32[]{:S(2)}) collective-permute-start(bf16[2,128,1408]{2,1,0:T(8,128)(2,1)S(1)} %shard_map.107.refs_0_.refs_1_), channel_id=1, source_target_pairs={{0,1},{1,0},{2,3},{3,2},{4,5},{5,4},{6,7},{7,6},{8,9},{9,8},{10,11... | collective-permute-start | bytes 2162696 | tf_op jit(solution)/shard_map/ppermute | solution.py:330
  71.6 1.2 shard_map.103
  72.8 0.9 slice.17
  73.8 0.0 copy-start.1
  73.8 0.0 copy-start.3
  73.8 0.0 copy-start.8
  73.8 4.0 %collective-permute-done.3.a_ref = bf16[128,640]{1,0:T(8,128)(2,1)S(1)} collective-permute-done((bf16[128,640]{1,0:T(8,128)(2,1)S(1)}, bf16[128,640]{1,0:T(8,128)(2,1)S(1)}, u32[]{:S(2)}, u32[]{:S(2)}) %collective-permute-start.3) | collective-permute-done | bytes 163872 | tf_op jit(solution)/shard_map/ppermute | solution.py:326
  77.8 4.1 %shard_map.117 = (f32[20,64,128]{2,1,0:T(8,128)S(1)}, f32[20,64,128]{2,1,0:T(8,128)S(1)}, f32[20,64,128]{2,1,0:T(8,128)S(1)}, f32[20,64,128]{2,1,0:T(8,128)S(1)}...) custom-call(s32[160,64]{1,0:T(8,128)S(1)} %copy.11.sel_ref, ...), custom_call_target="tpu_custom_call" | custom-call | flops 1000000000 | tf_op jit(solution)/shard_map/pallas_call | solution.py:59
  81.9 2.6 %shard_map.114.in_ref = f32[256,2560]{1,0:T(8,128)S(1)} custom-call(bf16[256,2048]{1,0:T(8,128)(2,1)S(1)} %get-tuple-element.24.xt_ref, bf16[256,2560]{1,0:T(8,128)(2,1)S(1)} %bitcast.18, bf16[128,1408]{1,0:T(8,128)(2,1)S(1)} %copy-done.5, bf16[2,128,1408]{2,1,0:T(8,128)(2,1)S(1)} %shard_map.109.refs_3_.refs_1_, bf16[128,1408]{1,0:T(8,128)(2,1)S(1)} %copy-done.7, ...), custom_call_target="tpu_custom_call" | custom-call | flops 1000000000 | tf_op jit(solution)/shard_map/pallas_call | solution.py:59
  84.5 2.4 %shard_map.110.refs_4_ = bf16[2048,256]{1,0:T(8,128)(2,1)S(1)} custom-call(s32[16]{0:T(128)S(1)} %copy-done.11, bf16[2560,256]{1,0:T(8,128)(2,1)S(1)} %get-tuple-element.21.wt_ref, bf16[128,1408]{1,0:T(8,128)(2,1)S(1)} %copy-done.5, bf16[2,128,1152]{2,1,0:T(8,128)(2,1)S(1)} %copy-done.1, bf16[128,1408]{1,0:T(8,128)(2,1)S(1)} %copy-done.7, ...), custom_call_target="tpu_custom_call" | custom-call | flops 1000000000 | tf_op jit(solution)/shard_map/pallas_call | solution.py:59
  87.0 0.6 collective-permute-start.17
  87.5 1.5 %collective-permute-start.12 = (bf16[2,128,640]{2,1,0:T(8,128)(2,1)S(1)}, bf16[2,128,640]{2,1,0:T(8,128)(2,1)S(1)}, u32[]{:S(2)}, u32[]{:S(2)}) collective-permute-start(bf16[2,128,640]{2,1,0:T(8,128)(2,1)S(1)} %slice.18), channel_id=1, source_target_pairs={{0,2},{2,4},{4,6},{6,8},{8,10},{10,12},{12,14},{14,0},{1,3},{3,5},... | collective-permute-start | bytes 983048 | tf_op jit(solution)/shard_map/ppermute | solution.py:326
  89.1 3.3 %shard_map.115.in_ref = f32[256,2560]{1,0:T(8,128)S(1)} custom-call(bf16[256,2048]{1,0:T(8,128)(2,1)S(1)} %get-tuple-element.24.xt_ref, f32[256,2560]{1,0:T(8,128)S(1)} %shard_map.114.in_ref, bf16[2,128,1408]{2,1,0:T(8,128)(2,1)S(1)} %shard_map.108.refs_0_, bf16[2,128,1408]{2,1,0:T(8,128)(2,1)S(1)} %shard_map.107.refs_0_.refs_1_, ...), custom_call_target="tpu_custom_call" | custom-call | flops 1000000000 | tf_op jit(solution)/shard_map/pallas_call | solution.py:59
  92.4 1.5 %collective-permute-start.16 = (bf16[2,128,512]{2,1,0:T(8,128)(2,1)S(1)}, bf16[2,128,512]{2,1,0:T(8,128)(2,1)S(1)}, u32[]{:S(2)}, u32[]{:S(2)}) collective-permute-start(bf16[2,128,512]{2,1,0:T(8,128)(2,1)S(1)} %slice.19), channel_id=1, source_target_pairs={{0,14},{2,0},{4,2},{6,4},{8,6},{10,8},{12,10},{14,12},{1,15},{3,1}... | collective-permute-start | bytes 786440 | tf_op jit(solution)/shard_map/ppermute | solution.py:326
  93.9 2.2 %shard_map.111.refs_4_ = bf16[2048,256]{1,0:T(8,128)(2,1)S(1)} custom-call(s32[16]{0:T(128)S(1)} %copy-done.11, bf16[2560,256]{1,0:T(8,128)(2,1)S(1)} %get-tuple-element.21.wt_ref, bf16[2,128,1408]{2,1,0:T(8,128)(2,1)S(1)} %shard_map.108.refs_0_, bf16[2,128,1152]{2,1,0:T(8,128)(2,1)} %collective-permute-done.10.refs_1_.refs_4_, ...), custom_call_target="tpu_custom_call" | custom-call | flops 1000000000 | tf_op jit(solution)/shard_map/pallas_call | solution.py:59
  96.2 0.7 shard_map.116.in_ref
  96.9 1.5 %shard_map.112.refs_4_ = bf16[2048,256]{1,0:T(8,128)(2,1)S(1)} custom-call(s32[16]{0:T(128)S(1)} %copy-done.11, bf16[2560,256]{1,0:T(8,128)(2,1)S(1)} %get-tuple-element.21.wt_ref, bf16[2,128,1408]{2,1,0:T(8,128)(2,1)S(1)} %shard_map.107.refs_0_.refs_1_, bf16[2,128,1152]{2,1,0:T(8,128)(2,1)S(1)} %collective-permute-done.11.refs_1_, ...), custom_call_target="tpu_custom_call" | custom-call | flops 1000000000 | tf_op jit(solution)/shard_map/pallas_call | solution.py:59
  98.4 3.0 %shard_map.118 = (f32[256,2560]{1,0:T(8,128)S(1)}, f32[80,128]{1,0:T(8,128)S(1)}) custom-call(bf16[256,2048]{1,0:T(8,128)(2,1)S(1)} %get-tuple-element.24.xt_ref, f32[256,2560]{1,0:T(8,128)S(1)} %shard_map.116.in_ref, f32[20,64,128]{2,1,0:T(8,128)S(1)} %get-tuple-element.25.refs_0_, f32[20,64,128]{2,1,0:T(8,128)S(1)} %get-tuple-element.26.refs_1_, ...), custom_call_target="tpu_custom_call" | custom-call | flops 1000000000 | tf_op jit(solution)/shard_map/pallas_call | solution.py:59
  101.4 9.1 %collective-permute-start.24 = (f32[80,128]{1,0:T(8,128)S(1)}, f32[80,128]{1,0:T(8,128)S(1)}, u32[]{:S(2)}, u32[]{:S(2)}) collective-permute-start(f32[80,128]{1,0:T(8,128)S(1)} %get-tuple-element.34.sent_ref), channel_id=1, source_target_pairs={{0,48},{16,32},{32,16},{48,0},{1,49},{17,33},{33,17},{49,1},{2,50}... | collective-permute-start | bytes 122888 | tf_op jit(solution)/shard_map/ppermute | solution.py:339
  110.5 0.3 collective-permute-start.23
  110.8 0.2 collective-permute-start.22
  111.0 3.1 %shard_map.119 = bf16[256,2560]{1,0:T(8,128)(2,1)} custom-call(f32[256,2560]{1,0:T(8,128)S(1)} %get-tuple-element.33.acc_ref, f32[80,128]{1,0:T(8,128)S(1)} %get-tuple-element.34.sent_ref, f32[20,64,128]{2,1,0:T(8,128)S(1)} %get-tuple-element.25.refs_0_, f32[20,64,128]{2,1,0:T(8,128)S(1)} %get-tuple-element.26.refs_1_, ...), custom_call_target="tpu_custom_call" | custom-call | flops 1000000000 | tf_op jit(solution)/shard_map/pallas_call | solution.py:59
  114.0 0.8 collective-permute-done.23
  114.8 2.6 %collective-permute-start.27 = (f32[80,128]{1,0:T(8,128)S(1)}, f32[80,128]{1,0:T(8,128)S(1)}, u32[]{:S(2)}, u32[]{:S(2)}) collective-permute-start(f32[80,128]{1,0:T(8,128)S(1)} %add_add_fusion.1), channel_id=1, source_target_pairs={{0,192},{64,0},{128,64},{192,128},{1,193},{65,1},{129,65},{193,129... | collective-permute-start | bytes 122888 | tf_op jit(solution)/shard_map/ppermute | solution.py:336
  117.4 1.7 %collective-permute-start.25 = (f32[80,128]{1,0:T(8,128)S(1)}, f32[80,128]{1,0:T(8,128)S(1)}, u32[]{:S(2)}, u32[]{:S(2)}) collective-permute-start(f32[80,128]{1,0:T(8,128)S(1)} %add_add_fusion.1), channel_id=1, source_target_pairs={{0,128},{64,192},{128,0},{192,64},{1,129},{65,193},{129,1},{193,65... | collective-permute-start | bytes 122888 | tf_op jit(solution)/shard_map/ppermute | solution.py:336
  119.1 2.1 %shard_map.113 = bf16[2048,256]{1,0:T(8,128)(2,1)} custom-call(s32[16]{0:T(128)S(1)} %copy-done.11, bf16[2560,256]{1,0:T(8,128)(2,1)S(1)} %get-tuple-element.21.wt_ref, bf16[128,1408]{1,0:T(8,128)(2,1)S(1)} %shard_map.105.refs_0_, bf16[2,128,640]{2,1,0:T(8,128)(2,1)S(1)} %collective-permute-done.12.refs_1_.refs_10_, ...), custom_call_target="tpu_custom_call" | custom-call | flops 1000000000 | tf_op jit(solution)/shard_map/pallas_call | solution.py:59
  121.2 1.6 %collective-permute-done.26 = f32[80,128]{1,0:T(8,128)S(1)} collective-permute-done((f32[80,128]{1,0:T(8,128)S(1)}, f32[80,128]{1,0:T(8,128)S(1)}, u32[]{:S(2)}, u32[]{:S(2)}) %collective-permute-start.26) | collective-permute-done | bytes 40992 | tf_op jit(solution)/shard_map/ppermute | solution.py:336
  122.8 3.1 %shard_map.120 = bf16[256,2560]{1,0:T(8,128)(2,1)} custom-call(f32[80,128]{1,0:T(8,128)S(1)} %add_add_fusion.s_ref, f32[20,64,128]{2,1,0:T(8,128)S(1)} %get-tuple-element.25.refs_0_, f32[20,64,128]{2,1,0:T(8,128)S(1)} %get-tuple-element.26.refs_1_, f32[20,64,128]{2,1,0:T(8,128)S(1)} %get-tuple-element.27.refs_2_, ...), custom_call_target="tpu_custom_call" | custom-call | flops 1000000000 | tf_op jit(solution)/shard_map/pallas_call | solution.py:59
  (54 shorter events, 0.3 us)
Async XLA Ops:
  0.6 1.1 copy-start.14
  1.8 16.0 %copy-start.4 = (bf16[128,1408]{1,0:T(8,128)(2,1)}, bf16[128,1408]{1,0:T(8,128)(2,1)S(1)}, u32[]{:S(2)}) copy-start(bf16[128,1408]{1,0:T(8,128)(2,1)S(1)} %get-tuple-element.22.refs_0_) | copy-start | bytes 1081348
  1.8 7.8 %collective-permute-start.8 = (bf16[128,1152]{1,0:T(8,128)(2,1)S(1)}, bf16[128,1152]{1,0:T(8,128)(2,1)S(1)}, u32[]{:S(2)}, u32[]{:S(2)}) collective-permute-start(bf16[128,1152]{1,0:T(8,128)(2,1)S(1)} %get-tuple-element.23.a_ref), channel_id=1, source_target_pairs={{0,1},{1,0},{2,3},{3,2},{4,5},{5,4},{6,7},{7,6},{8,9},{9,8},{10,11... | collective-permute-start | bytes 884744 | tf_op jit(solution)/shard_map/ppermute | solution.py:330
  4.0 15.1 %collective-permute-start = (bf16[128,1408]{1,0:T(8,128)(2,1)S(1)}, bf16[128,1408]{1,0:T(8,128)(2,1)S(1)}, u32[]{:S(2)}, u32[]{:S(2)}) collective-permute-start(bf16[128,1408]{1,0:T(8,128)(2,1)S(1)} %get-tuple-element.22.refs_0_), channel_id=1, source_target_pairs={{0,2},{2,4},{4,6},{6,8},{8,10},{10,12},{12,14},{14,0},{1,3},{3,5},... | collective-permute-start | bytes 1081352 | tf_op jit(solution)/shard_map/ppermute | solution.py:326
  9.6 29.1 %copy-start = (bf16[2,128,1152]{2,1,0:T(8,128)(2,1)}, bf16[2,128,1152]{2,1,0:T(8,128)(2,1)S(1)}, u32[]{:S(2)}) copy-start(bf16[2,128,1152]{2,1,0:T(8,128)(2,1)S(1)} %shard_map.106.refs_1_.refs_3_) | copy-start | bytes 1769476
  9.6 30.5 %collective-permute-start.9 = (bf16[2,128,1152]{2,1,0:T(8,128)(2,1)S(1)}, bf16[2,128,1152]{2,1,0:T(8,128)(2,1)S(1)}, u32[]{:S(2)}, u32[]{:S(2)}) collective-permute-start(bf16[2,128,1152]{2,1,0:T(8,128)(2,1)S(1)} %shard_map.106.refs_1_.refs_3_), channel_id=1, source_target_pairs={{0,2},{2,4},{4,6},{6,8},{8,10},{10,12},{12,14},{14,0},{1,3},{3,5},... | collective-permute-start | bytes 1769480 | tf_op jit(solution)/shard_map/ppermute | solution.py:326
  12.4 27.8 %collective-permute-start.13 = (bf16[2,128,1152]{2,1,0:T(8,128)(2,1)S(1)}, bf16[2,128,1152]{2,1,0:T(8,128)(2,1)}, u32[]{:S(2)}, u32[]{:S(2)}) collective-permute-start(bf16[2,128,1152]{2,1,0:T(8,128)(2,1)S(1)} %shard_map.106.refs_1_.refs_3_), channel_id=1, source_target_pairs={{0,14},{2,0},{4,2},{6,4},{8,6},{10,8},{12,10},{14,12},{1,15},{3,1}... | collective-permute-start | bytes 1769480 | tf_op jit(solution)/shard_map/ppermute | solution.py:326
  16.4 18.9 %collective-permute-start.4 = (bf16[128,1408]{1,0:T(8,128)(2,1)S(1)}, bf16[128,1408]{1,0:T(8,128)(2,1)S(1)}, u32[]{:S(2)}, u32[]{:S(2)}) collective-permute-start(bf16[128,1408]{1,0:T(8,128)(2,1)S(1)} %get-tuple-element.22.refs_0_), channel_id=1, source_target_pairs={{0,14},{2,0},{4,2},{6,4},{8,6},{10,8},{12,10},{14,12},{1,15},{3,1}... | collective-permute-start | bytes 1081352 | tf_op jit(solution)/shard_map/ppermute | solution.py:326
  17.8 21.0 %collective-permute-start.20 = (bf16[128,1408]{1,0:T(8,128)(2,1)S(1)}, bf16[128,1408]{1,0:T(8,128)(2,1)S(1)}, u32[]{:S(2)}, u32[]{:S(2)}) collective-permute-start(bf16[128,1408]{1,0:T(8,128)(2,1)S(1)} %get-tuple-element.22.refs_0_), channel_id=1, source_target_pairs={{0,1},{1,0},{2,3},{3,2},{4,5},{5,4},{6,7},{7,6},{8,9},{9,8},{10,11... | collective-permute-start | bytes 1081352 | tf_op jit(solution)/shard_map/ppermute | solution.py:330
  19.1 23.8 %collective-permute-start.1 = (bf16[128,1408]{1,0:T(8,128)(2,1)S(1)}, bf16[128,1408]{1,0:T(8,128)(2,1)S(1)}, u32[]{:S(2)}, u32[]{:S(2)}) collective-permute-start(bf16[128,1408]{1,0:T(8,128)(2,1)S(1)} %collective-permute-done.a_ref), channel_id=1, source_target_pairs={{0,2},{2,4},{4,6},{6,8},{8,10},{10,12},{12,14},{14,0},{1,3},{3,5},... | collective-permute-start | bytes 1081352 | tf_op jit(solution)/shard_map/ppermute | solution.py:326
  35.3 8.8 %collective-permute-start.5 = (bf16[128,1408]{1,0:T(8,128)(2,1)S(1)}, bf16[128,1408]{1,0:T(8,128)(2,1)}, u32[]{:S(2)}, u32[]{:S(2)}) collective-permute-start(bf16[128,1408]{1,0:T(8,128)(2,1)S(1)} %collective-permute-done.4.b_ref), channel_id=1, source_target_pairs={{0,14},{2,0},{4,2},{6,4},{8,6},{10,8},{12,10},{14,12},{1,15},{3,1}... | collective-permute-start | bytes 1081352 | tf_op jit(solution)/shard_map/ppermute | solution.py:326
  38.7 9.9 %copy-start.6 = (bf16[128,1408]{1,0:T(8,128)(2,1)}, bf16[128,1408]{1,0:T(8,128)(2,1)S(1)}, u32[]{:S(2)}) copy-start(bf16[128,1408]{1,0:T(8,128)(2,1)S(1)} %collective-permute-done.20.refs_2_) | copy-start | bytes 1081348
  38.8 31.4 %collective-permute-start.21 = (bf16[2,128,1408]{2,1,0:T(8,128)(2,1)S(1)}, bf16[2,128,1408]{2,1,0:T(8,128)(2,1)S(1)}, u32[]{:S(2)}, u32[]{:S(2)}) collective-permute-start(bf16[2,128,1408]{2,1,0:T(8,128)(2,1)S(1)} %shard_map.109.refs_3_.refs_1_), channel_id=1, source_target_pairs={{0,1},{1,0},{2,3},{3,2},{4,5},{5,4},{6,7},{7,6},{8,9},{9,8},{10,11... | collective-permute-start | bytes 2162696 | tf_op jit(solution)/shard_map/ppermute | solution.py:330
  40.1 8.5 %copy-start.2 = (bf16[2,128,1152]{2,1,0:T(8,128)(2,1)}, bf16[2,128,1152]{2,1,0:T(8,128)(2,1)S(1)}, u32[]{:S(2)}) copy-start(bf16[2,128,1152]{2,1,0:T(8,128)(2,1)S(1)} %collective-permute-done.9.refs_4_) | copy-start | bytes 1769476
  40.1 21.1 %collective-permute-start.10 = (bf16[2,128,1152]{2,1,0:T(8,128)(2,1)S(1)}, bf16[2,128,1152]{2,1,0:T(8,128)(2,1)}, u32[]{:S(2)}, u32[]{:S(2)}) collective-permute-start(bf16[2,128,1152]{2,1,0:T(8,128)(2,1)S(1)} %collective-permute-done.9.refs_4_), channel_id=1, source_target_pairs={{0,2},{2,4},{4,6},{6,8},{8,10},{10,12},{12,14},{14,0},{1,3},{3,5},... | collective-permute-start | bytes 1769480 | tf_op jit(solution)/shard_map/ppermute | solution.py:326
  40.2 24.8 %collective-permute-start.14 = (bf16[2,128,1152]{2,1,0:T(8,128)(2,1)}, bf16[2,128,1152]{2,1,0:T(8,128)(2,1)}, u32[]{:S(2)}, u32[]{:S(2)}) collective-permute-start(bf16[2,128,1152]{2,1,0:T(8,128)(2,1)} %collective-permute-done.13.refs_6_.refs_5_), channel_id=1, source_target_pairs={{0,14},{2,0},{4,2},{6,4},{8,6},{10,8},{12,10},{14,12},{1,15},{3,1}... | collective-permute-start | bytes 1769480 | tf_op jit(solution)/shard_map/ppermute | solution.py:326
  42.8 18.2 %collective-permute-start.2 = (bf16[128,1408]{1,0:T(8,128)(2,1)S(1)}, bf16[128,1408]{1,0:T(8,128)(2,1)S(1)}, u32[]{:S(2)}, u32[]{:S(2)}) collective-permute-start(bf16[128,1408]{1,0:T(8,128)(2,1)S(1)} %collective-permute-done.1.a_ref), channel_id=1, source_target_pairs={{0,2},{2,4},{4,6},{6,8},{8,10},{10,12},{12,14},{14,0},{1,3},{3,5},... | collective-permute-start | bytes 1081352 | tf_op jit(solution)/shard_map/ppermute | solution.py:326
  44.1 20.5 %collective-permute-start.6 = (bf16[128,1408]{1,0:T(8,128)(2,1)}, bf16[128,1408]{1,0:T(8,128)(2,1)}, u32[]{:S(2)}, u32[]{:S(2)}) collective-permute-start(bf16[128,1408]{1,0:T(8,128)(2,1)} %collective-permute-done.5.b_ref), channel_id=1, source_target_pairs={{0,14},{2,0},{4,2},{6,4},{8,6},{10,8},{12,10},{14,12},{1,15},{3,1}... | collective-permute-start | bytes 1081352 | tf_op jit(solution)/shard_map/ppermute | solution.py:326
  61.0 0.7 copy-start.9
  61.0 28.1 %collective-permute-start.19 = (bf16[2,128,1408]{2,1,0:T(8,128)(2,1)S(1)}, bf16[2,128,1408]{2,1,0:T(8,128)(2,1)S(1)}, u32[]{:S(2)}, u32[]{:S(2)}) collective-permute-start(bf16[2,128,1408]{2,1,0:T(8,128)(2,1)S(1)} %shard_map.108.refs_0_), channel_id=1, source_target_pairs={{0,1},{1,0},{2,3},{3,2},{4,5},{5,4},{6,7},{7,6},{8,9},{9,8},{10,11... | collective-permute-start | bytes 2162696 | tf_op jit(solution)/shard_map/ppermute | solution.py:330
  61.8 25.8 %collective-permute-start.11 = (bf16[2,128,1152]{2,1,0:T(8,128)(2,1)}, bf16[2,128,1152]{2,1,0:T(8,128)(2,1)S(1)}, u32[]{:S(2)}, u32[]{:S(2)}) collective-permute-start(bf16[2,128,1152]{2,1,0:T(8,128)(2,1)} %collective-permute-done.10.refs_1_.refs_4_), channel_id=1, source_target_pairs={{0,2},{2,4},{4,6},{6,8},{8,10},{10,12},{12,14},{14,0},{1,3},{3,5},... | collective-permute-start | bytes 1769480 | tf_op jit(solution)/shard_map/ppermute | solution.py:326
  63.4 8.2 %copy-start.11 = (s32[16]{0:T(128)S(1)}, s32[16]{0:T(128)}, u32[]{:S(2)}) copy-start(s32[16]{0:T(128)} %stack.67.idx_ref) | copy-start | bytes 196
  64.5 13.2 %collective-permute-start.3 = (bf16[128,640]{1,0:T(8,128)(2,1)S(1)}, bf16[128,640]{1,0:T(8,128)(2,1)S(1)}, u32[]{:S(2)}, u32[]{:S(2)}) collective-permute-start(bf16[128,640]{1,0:T(8,128)(2,1)S(1)} %slice.16), channel_id=1, source_target_pairs={{0,2},{2,4},{4,6},{6,8},{8,10},{10,12},{12,14},{14,0},{1,3},{3,5},... | collective-permute-start | bytes 491528 | tf_op jit(solution)/shard_map/ppermute | solution.py:326
  65.0 27.4 %collective-permute-start.15 = (bf16[2,128,1152]{2,1,0:T(8,128)(2,1)}, bf16[2,128,1152]{2,1,0:T(8,128)(2,1)S(1)}, u32[]{:S(2)}, u32[]{:S(2)}) collective-permute-start(bf16[2,128,1152]{2,1,0:T(8,128)(2,1)} %collective-permute-done.14.refs_3_.refs_5_), channel_id=1, source_target_pairs={{0,14},{2,0},{4,2},{6,4},{8,6},{10,8},{12,10},{14,12},{1,15},{3,1}... | collective-permute-start | bytes 1769480 | tf_op jit(solution)/shard_map/ppermute | solution.py:326
  67.9 1.0 copy-start.10
  68.9 2.6 %copy-start.12 = (bf16[256,2560]{1,0:T(8,128)(2,1)S(1)}, bf16[256,2560]{1,0:T(8,128)(2,1)}, u32[]{:S(2)}) copy-start(bf16[256,2560]{1,0:T(8,128)(2,1)} %w_ref.1) | copy-start | bytes 3932164
  68.9 2.6 %copy-start.13 = (bf16[2048,256]{1,0:T(8,128)(2,1)S(1)}, bf16[2048,256]{1,0:T(8,128)(2,1)}, u32[]{:S(2)}) copy-start(bf16[2048,256]{1,0:T(8,128)(2,1)} %x_ref.1) | copy-start | bytes 3145732
  70.1 7.7 %copy-start.15 = (bf16[128,256]{1,0:T(8,128)(2,1)S(1)}, bf16[128,256]{1,0:T(8,128)(2,1)}, u32[]{:S(2)}) copy-start(bf16[128,256]{1,0:T(8,128)(2,1)} %constant.133.clone.g2_ref) | copy-start | bytes 196612
  70.1 7.6 %copy-start.16 = (bf16[128,64]{1,0:T(8,128)(2,1)S(1)}, bf16[128,64]{1,0:T(8,128)(2,1)}, u32[]{:S(2)}) copy-start(bf16[128,64]{1,0:T(8,128)(2,1)} %constant.132.clone.t2_ref) | copy-start | bytes 49156
  70.1 7.6 %copy-start.17 = (bf16[64,192]{1,0:T(8,128)(2,1)S(1)}, bf16[64,192]{1,0:T(8,128)(2,1)}, u32[]{:S(2)}) copy-start(bf16[64,192]{1,0:T(8,128)(2,1)} %constant.131.clone.tt_ref) | copy-start | bytes 73732
  70.2 26.7 %collective-permute-start.18 = (bf16[2,128,1408]{2,1,0:T(8,128)(2,1)S(1)}, bf16[2,128,1408]{2,1,0:T(8,128)(2,1)S(1)}, u32[]{:S(2)}, u32[]{:S(2)}) collective-permute-start(bf16[2,128,1408]{2,1,0:T(8,128)(2,1)S(1)} %shard_map.107.refs_0_.refs_1_), channel_id=1, source_target_pairs={{0,1},{1,0},{2,3},{3,2},{4,5},{5,4},{6,7},{7,6},{8,9},{9,8},{10,11... | collective-permute-start | bytes 2162696 | tf_op jit(solution)/shard_map/ppermute | solution.py:330
  73.8 8.1 %copy-start.1 = (bf16[2,128,1152]{2,1,0:T(8,128)(2,1)S(1)}, bf16[2,128,1152]{2,1,0:T(8,128)(2,1)}, u32[]{:S(2)}) copy-start(bf16[2,128,1152]{2,1,0:T(8,128)(2,1)} %copy-done) | copy-start | bytes 1769476
  73.8 8.1 %copy-start.3 = (bf16[2,128,1152]{2,1,0:T(8,128)(2,1)S(1)}, bf16[2,128,1152]{2,1,0:T(8,128)(2,1)}, u32[]{:S(2)}) copy-start(bf16[2,128,1152]{2,1,0:T(8,128)(2,1)} %copy-done.2) | copy-start | bytes 1769476
  73.8 8.1 %copy-start.5 = (bf16[128,1408]{1,0:T(8,128)(2,1)S(1)}, bf16[128,1408]{1,0:T(8,128)(2,1)}, u32[]{:S(2)}) copy-start(bf16[128,1408]{1,0:T(8,128)(2,1)} %copy-done.4) | copy-start | bytes 1081348
  73.8 8.1 %copy-start.7 = (bf16[128,1408]{1,0:T(8,128)(2,1)S(1)}, bf16[128,1408]{1,0:T(8,128)(2,1)}, u32[]{:S(2)}) copy-start(bf16[128,1408]{1,0:T(8,128)(2,1)} %copy-done.6) | copy-start | bytes 1081348
  73.8 8.1 %copy-start.8 = (bf16[1,256,2560]{2,1,0:T(8,128)(2,1)S(1)}, bf16[1,256,2560]{2,1,0:T(8,128)(2,1)}, u32[]{:S(2)}) copy-start(bf16[1,256,2560]{2,1,0:T(8,128)(2,1)} %param.11) | copy-start | bytes 3932164
  77.8 9.1 %collective-permute-start.7 = (bf16[128,768]{1,0:T(8,128)(2,1)S(1)}, bf16[128,768]{1,0:T(8,128)(2,1)S(1)}, u32[]{:S(2)}, u32[]{:S(2)}) collective-permute-start(bf16[128,768]{1,0:T(8,128)(2,1)S(1)} %slice.17), channel_id=1, source_target_pairs={{0,14},{2,0},{4,2},{6,4},{8,6},{10,8},{12,10},{14,12},{1,15},{3,1}... | collective-permute-start | bytes 589832 | tf_op jit(solution)/shard_map/ppermute | solution.py:326
  87.0 11.4 %collective-permute-start.17 = (bf16[128,1408]{1,0:T(8,128)(2,1)S(1)}, bf16[128,1408]{1,0:T(8,128)(2,1)S(1)}, u32[]{:S(2)}, u32[]{:S(2)}) collective-permute-start(bf16[128,1408]{1,0:T(8,128)(2,1)S(1)} %shard_map.105.refs_0_), channel_id=1, source_target_pairs={{0,1},{1,0},{2,3},{3,2},{4,5},{5,4},{6,7},{7,6},{8,9},{9,8},{10,11... | collective-permute-start | bytes 1081352 | tf_op jit(solution)/shard_map/ppermute | solution.py:330
  87.5 10.9 %collective-permute-start.12 = (bf16[2,128,640]{2,1,0:T(8,128)(2,1)S(1)}, bf16[2,128,640]{2,1,0:T(8,128)(2,1)S(1)}, u32[]{:S(2)}, u32[]{:S(2)}) collective-permute-start(bf16[2,128,640]{2,1,0:T(8,128)(2,1)S(1)} %slice.18), channel_id=1, source_target_pairs={{0,2},{2,4},{4,6},{6,8},{8,10},{10,12},{12,14},{14,0},{1,3},{3,5},... | collective-permute-start | bytes 983048 | tf_op jit(solution)/shard_map/ppermute | solution.py:326
  92.4 6.0 %collective-permute-start.16 = (bf16[2,128,512]{2,1,0:T(8,128)(2,1)S(1)}, bf16[2,128,512]{2,1,0:T(8,128)(2,1)S(1)}, u32[]{:S(2)}, u32[]{:S(2)}) collective-permute-start(bf16[2,128,512]{2,1,0:T(8,128)(2,1)S(1)} %slice.19), channel_id=1, source_target_pairs={{0,14},{2,0},{4,2},{6,4},{8,6},{10,8},{12,10},{14,12},{1,15},{3,1}... | collective-permute-start | bytes 786440 | tf_op jit(solution)/shard_map/ppermute | solution.py:326
  101.4 12.6 %collective-permute-start.24 = (f32[80,128]{1,0:T(8,128)S(1)}, f32[80,128]{1,0:T(8,128)S(1)}, u32[]{:S(2)}, u32[]{:S(2)}) collective-permute-start(f32[80,128]{1,0:T(8,128)S(1)} %get-tuple-element.34.sent_ref), channel_id=1, source_target_pairs={{0,48},{16,32},{32,16},{48,0},{1,49},{17,33},{33,17},{49,1},{2,50}... | collective-permute-start | bytes 122888 | tf_op jit(solution)/shard_map/ppermute | solution.py:339
  110.5 4.4 %collective-permute-start.23 = (f32[80,128]{1,0:T(8,128)S(1)}, f32[80,128]{1,0:T(8,128)S(1)}, u32[]{:S(2)}, u32[]{:S(2)}) collective-permute-start(f32[80,128]{1,0:T(8,128)S(1)} %get-tuple-element.34.sent_ref), channel_id=1, source_target_pairs={{0,32},{32,0},{1,33},{33,1},{2,34},{34,2},{3,35},{35,3},{4,36},{36... | collective-permute-start | bytes 122888 | tf_op jit(solution)/shard_map/ppermute | solution.py:336
  110.8 4.0 %collective-permute-start.22 = (f32[80,128]{1,0:T(8,128)S(1)}, f32[80,128]{1,0:T(8,128)S(1)}, u32[]{:S(2)}, u32[]{:S(2)}) collective-permute-start(f32[80,128]{1,0:T(8,128)S(1)} %get-tuple-element.34.sent_ref), channel_id=1, source_target_pairs={{0,16},{16,0},{1,17},{17,1},{2,18},{18,2},{3,19},{19,3},{4,20},{20... | collective-permute-start | bytes 122888 | tf_op jit(solution)/shard_map/ppermute | solution.py:336
  114.8 6.4 %collective-permute-start.27 = (f32[80,128]{1,0:T(8,128)S(1)}, f32[80,128]{1,0:T(8,128)S(1)}, u32[]{:S(2)}, u32[]{:S(2)}) collective-permute-start(f32[80,128]{1,0:T(8,128)S(1)} %add_add_fusion.1), channel_id=1, source_target_pairs={{0,192},{64,0},{128,64},{192,128},{1,193},{65,1},{129,65},{193,129... | collective-permute-start | bytes 122888 | tf_op jit(solution)/shard_map/ppermute | solution.py:336
  117.4 5.4 %collective-permute-start.26 = (f32[80,128]{1,0:T(8,128)S(1)}, f32[80,128]{1,0:T(8,128)S(1)}, u32[]{:S(2)}, u32[]{:S(2)}) collective-permute-start(f32[80,128]{1,0:T(8,128)S(1)} %add_add_fusion.1), channel_id=1, source_target_pairs={{0,64},{64,128},{128,192},{192,0},{1,65},{65,129},{129,193},{193,1... | collective-permute-start | bytes 122888 | tf_op jit(solution)/shard_map/ppermute | solution.py:336
  117.4 5.4 %collective-permute-start.25 = (f32[80,128]{1,0:T(8,128)S(1)}, f32[80,128]{1,0:T(8,128)S(1)}, u32[]{:S(2)}, u32[]{:S(2)}) collective-permute-start(f32[80,128]{1,0:T(8,128)S(1)} %add_add_fusion.1), channel_id=1, source_target_pairs={{0,128},{64,192},{128,0},{192,64},{1,129},{65,193},{129,1},{193,65... | collective-permute-start | bytes 122888 | tf_op jit(solution)/shard_map/ppermute | solution.py:336
where the time goes:
time: 126 us
  starting transfers between devices  46.8 us (37%)
  waiting for transfers between devices  40.2 us (32%)
  Pallas kernels  31.6 us (25%)
  local copies, waits for them, and re-layouts  6.24 us (5%)
    ppermute x16, waiting for transfers between devices, zp(): return lax.ppermute(x, 'z', [(i, (i + step) % n) for i in range(n)])  33.9 us
    pallas_call x18, Pallas kernels, call(): pl.pallas_call(kernel, out_shape=out, in_specs=specs, out_specs=vmem(len(...  31.6 us
    ppermute x16, starting transfers between devices, zp(): return lax.ppermute(x, 'z', [(i, (i + step) % n) for i in range(n)])  25.9 us
    ppermute x1, starting transfers between devices, over_replicas(): b = lax.ppermute(s, ('yh', 'core'), [(i, i ^ 3) for i in range(4)])  9.06 us
    ppermute x6, starting transfers between devices, yp(): return lax.ppermute(x, 'yl', [(0, 1), (1, 0)])  6.98 us
    ppermute x5, starting transfers between devices, shift(): return lax.ppermute(v, axis, [(i, (i + step) % n) for i in range(n)])  4.79 us
    ppermute x6, waiting for transfers between devices, yp(): return lax.ppermute(x, 'yl', [(0, 1), (1, 0)])  3.93 us
    unnamed x37, local copies, waits for them, and re-layouts  3.64 us
  transfers between devices with their start and end apart: 28, of which 8 were waited for; matrix products, arithmetic and copies ran while one was open for 3% of the time, Pallas kernels for 20%

commit v1 on v0

--- a/solution.py
+++ b/solution.py
@@ -146,16 +146,30 @@
     return (y[:n, :128] + y[n:, :128]) + (y[:n, 128:] + y[n:, 128:])
 
 
-def over_pairs(brows, pcols, run):
+def over_pairs(brows, first, last, run, at_once=None):
+    cut = CUT // 128
+
+    def number(r, cp):
+        start, end = (0, cut) if first < cut else (cut, last)
+        return start * brows + r * (end - start) + cp - start
+
+    def some(cps):
+        for cp in cps:
+            at = cp * 128 if isinstance(cp, int) else pl.multiple_of(cp * 128, 128)
+            for r in range(brows):
+                run(r, cp, number(r, cp), slice(r * BLK, (r + 1) * BLK), pl.ds(at, 128))
+
+    if at_once is None:
+        some(range(first, last))
+        return
+
     def group(g, _):
-        for i in range(5):
-            cp = g * 5 + i
-            at = pl.ds(pl.multiple_of(cp * 128, 128), 128)
-            for r in range(brows):
-                run(r, cp, r * pcols + cp, slice(r * BLK, (r + 1) * BLK), at)
+        some([first + g * at_once + i for i in range(at_once)])
         return 0
 
-    lax.fori_loop(0, pcols // 5, group, 0)
+    whole = (last - first) // at_once
+    lax.fori_loop(0, whole, group, 0)
+    some(range(first + whole * at_once, last))
 
 
 def distinct(pieces):
@@ -237,60 +251,70 @@
     return call(kernel, shape((a.shape[0], m + b.shape[1]), a.dtype), (a, b), vmem(2))
 
 
-def wgrad_encode(xt, acc, pieces, rts, cts, scale):
-    arrays, pieces = distinct(pieces)
+def wgrad_encode(xt, acc, pieces, rts, cts, scale, before):
     rows, cols = acc.shape
     brows = rows // BLK
-    pcols = cols // 128
+    arrays, pieces = distinct(pieces)
+    lo, hi = (0, CUT) if before is None else (CUT, cols)
+    pieces = [(w, sub, slot, slots, c - lo, n) for w, sub, slot, slots, c, n in pieces]
+    given = [] if before is None else [before]
+    m = hi // 128 * brows
 
     def kernel(xt_ref, in_ref, *refs):
         rt, ct = refs[:brows], refs[brows:2 * brows]
         *ins, acc_ref, sent_ref = refs[2 * brows:]
-        wgrad_into(acc_ref, lambda at, n: in_ref[:, at:at + n], xt_ref, pieces, ins, scale)
+        wgrad_into(acc_ref, lambda at, n: in_ref[:, lo + at:lo + at + n], xt_ref, pieces, ins, scale)
+        if given:
+            sent_ref[:lo // 128 * brows, :] = ins[-1][...]
 
         def one(r, cp, p, at, cols_at):
-            u = product(acc_ref[at, cols_at], ct[r][cp])
-            sent_ref[pl.ds(p, 1), :] = jnp.sum(u * rt[r][cp], axis=0, keepdims=True)
-
-        over_pairs(brows, pcols, one)
+            u = product(acc_ref[at, cp * 128 - lo:cp * 128 - lo + 128], ct[r][cp])
+            sent_ref[p:p + 1, :] = jnp.sum(u * rt[r][cp], axis=0, keepdims=True)
+
+        over_pairs(brows, lo // 128, hi // 128, one)
 
     return call(
         kernel,
-        [shape(acc.shape, jnp.float32), shape((brows * pcols, 128), jnp.float32)],
-        (xt, acc, *rts, *cts, *arrays),
-        vmem(2 + 2 * brows + len(arrays)),
+        [shape((rows, hi - lo), jnp.float32), shape((m, 128), jnp.float32)],
+        (xt, acc, *rts, *cts, *arrays, *given),
+        vmem(2 + 2 * brows + len(arrays) + len(given)),
     )
 
 
-def residual(acc, sent, rts, cds):
-    rows, cols = acc.shape
-    pcols = cols // 128
+def residual(accs, sent, rts, cds):
+    rows = accs[0].shape[0]
+    cols = sum(x.shape[1] for x in accs)
     brows = rows // BLK
 
-    def kernel(acc_ref, sent_ref, *refs):
+    def kernel(a_ref, b_ref, sent_ref, *refs):
         rt, cd, out_ref = refs[:brows], refs[brows:2 * brows], refs[-1]
 
-        def one(r, cp, p, at, cols_at):
-            e = product(rt[r][cp] * sent_ref[pl.ds(p, 1), :], cd[r][cp])
-            out_ref[at, cols_at] = (acc_ref[at, cols_at] - e).astype(jnp.bfloat16)
-
-        over_pairs(brows, pcols, one)
-
-    return call(kernel, shape(acc.shape, jnp.bfloat16), (acc, sent, *rts, *cds), vmem(2 + 2 * brows))
+        def walk(acc_ref, lo, hi):
+            def one(r, cp, p, at, cols_at):
+                e = product(rt[r][cp] * sent_ref[pl.ds(p, 1), :], cd[r][cp])
+                here = pl.ds(pl.multiple_of(cp * 128 - lo, 128), 128)
+                out_ref[at, cols_at] = (acc_ref[at, here] - e).astype(jnp.bfloat16)
+
+            over_pairs(brows, lo // 128, hi // 128, one, 3)
+
+        walk(a_ref, 0, CUT)
+        walk(b_ref, CUT, cols)
+
+    return call(kernel, shape((rows, cols), jnp.bfloat16), (*accs, sent, *rts, *cds), vmem(3 + 2 * brows))
 
 
 def decode_update(total, rts, cds, rows, cols, factor):
-    pcols = cols // 128
     brows = rows // BLK
 
     def kernel(s_ref, *refs):
         rt, cd, out_ref = refs[:brows], refs[brows:2 * brows], refs[-1]
 
         def one(r, cp, p, at, cols_at):
-            e = product(rt[r][cp] * (s_ref[pl.ds(p, 1), :] * factor), cd[r][cp])
+            e = product(rt[r][cp] * (s_ref[p:p + 1, :] * factor), cd[r][cp])
             out_ref[at, cols_at] = e.astype(jnp.bfloat16)
 
-        over_pairs(brows, pcols, one)
+        over_pairs(brows, 0, CUT // 128, one)
+        over_pairs(brows, CUT // 128, cols // 128, one)
 
     return call(kernel, shape((rows, cols), jnp.bfloat16), (total, *rts, *cds), vmem(1 + 2 * brows))
 
@@ -396,7 +420,8 @@
     acc = wgrad_first(xt, momentum[0], w_pieces([("own", 0, 1, -1), ("other", 0), ("a", 0, 1, -1)]), scale)
     acc = wgrad_more(xt, acc, w_pieces([("own", 2, -2, 3, -3), ("other", 1, -1, 2, -2), ("a", 2, -2)]), scale)
     acc = wgrad_more(xt, acc, w_pieces([("own", 4), ("a", 3, -3)]), scale)
-    acc, sent = wgrad_encode(xt, acc, w_pieces([("other", 3, -3, 4), ("a", 4)]), rts, cts, scale)
+    acc_a, sent_a = wgrad_encode(xt, acc, w_pieces([("a", 4)]), rts, cts, scale, None)
+    acc_b, sent = wgrad_encode(xt, acc, w_pieces([("other", 3, -3, 4)]), rts, cts, scale, sent_a)
     total = over_replicas(sent)
 
     def g_pieces(offsets):
@@ -411,7 +436,7 @@
     dacts = None
     for offsets in ((0, 1, -1), (2, -2), (3, -3), (4,)):
         dacts = input_grad(idx, wt, g_pieces(offsets), inputs.shape[0], dacts)
-    fresh = residual(acc, sent, rts, cds)
+    fresh = residual((acc_a, acc_b), sent, rts, cds)
     factor = BLK / math.sqrt(TOPK) / math.prod(lax.axis_size(a) for a in REPLICA)
     update = decode_update(total, rts, cds, rows, cols, factor)
     return dacts, fresh[None], update

time: 126 us -> 124 us (0.984)
  waiting for transfers between devices: 40.2 us -> 38.7 us
    ppermute x1, starting transfers between devices: 9.06 us -> 6.28 us  [over_replicas(): b = lax.ppermute(s, ('yh', 'core'), [(i, i ^ 3) for i in range(4)])]
    ppermute x5, starting transfers between devices: 4.79 us -> 7.01 us  [shift(): return lax.ppermute(v, axis, [(i, (i + step) % n) for i in range(n)])]
    ppermute x5, waiting for transfers between devices: 2.34 us -> 0.84 us  [shift(): return lax.ppermute(v, axis, [(i, (i + step) % n) for i in range(n)])]
    pallas_call x18 -> x19, Pallas kernels: 31.6 us -> 31 us  [call(): pl.pallas_call(kernel, out_shape=out, in_specs=specs, out_specs=vmem(len(...]
  transfers between devices with their start and end apart: 28 -> 28, of which waited for: 8 -> 7; matrix products, arithmetic and copies ran while one was open for 3% -> 3% of each run, Pallas kernels for 20% -> 22%
where the time goes in v1:
time: 124 us; the launch traced here: 123 us
  starting transfers between devices  46.2 us (37%)
  waiting for transfers between devices  38.7 us (31%)
  Pallas kernels  31 us (25%)
  local copies, waits for them, and re-layouts  6.23 us (5%)
    ppermute x16, waiting for transfers between devices, zp(): return lax.ppermute(x, 'z', [(i, (i + step) % n) for i in range(n)])  33.9 us
    pallas_call x19, Pallas kernels, call(): pl.pallas_call(kernel, out_shape=out, in_specs=specs, out_specs=vmem(len(...  31 us
    ppermute x16, starting transfers between devices, zp(): return lax.ppermute(x, 'z', [(i, (i + step) % n) for i in range(n)])  26 us
    ppermute x5, starting transfers between devices, shift(): return lax.ppermute(v, axis, [(i, (i + step) % n) for i in range(n)])  7.01 us
    ppermute x6, starting transfers between devices, yp(): return lax.ppermute(x, 'yl', [(0, 1), (1, 0)])  6.98 us
    ppermute x1, starting transfers between devices, over_replicas(): b = lax.ppermute(s, ('yh', 'core'), [(i, i ^ 3) for i in range(4)])  6.28 us
    ppermute x6, waiting for transfers between devices, yp(): return lax.ppermute(x, 'yl', [(0, 1), (1, 0)])  3.93 us
    unnamed x37, local copies, waits for them, and re-layouts  3.64 us
  transfers between devices with their start and end apart: 28, of which 7 were waited for; matrix products, arithmetic and copies ran while one was open for 3% of the time, Pallas kernels for 22%

profile of v1, /device:TPU:1, one launch (start us, length us, event | category | flops | bytes accessed | tf_op | source)
XLA Modules:
  0.0 123.2 jit_solution(16011089004817832405)
XLA Ops:
  0.6 1.1 copy-done.14
  1.8 2.2 %collective-permute-start.8 = (bf16[128,1152]{1,0:T(8,128)(2,1)S(1)}, bf16[128,1152]{1,0:T(8,128)(2,1)S(1)}, u32[]{:S(2)}, u32[]{:S(2)}) collective-permute-start(bf16[128,1152]{1,0:T(8,128)(2,1)S(1)} %get-tuple-element.25.a_ref), channel_id=1, source_target_pairs={{0,1},{1,0},{2,3},{3,2},{4,5},{5,4},{6,7},{7,6},{8,9},{9,8},{10,11... | collective-permute-start | bytes 884744 | tf_op jit(solution)/shard_map/ppermute | solution.py:354
  4.0 1.6 %collective-permute-start = (bf16[128,1408]{1,0:T(8,128)(2,1)S(1)}, bf16[128,1408]{1,0:T(8,128)(2,1)S(1)}, u32[]{:S(2)}, u32[]{:S(2)}) collective-permute-start(bf16[128,1408]{1,0:T(8,128)(2,1)S(1)} %get-tuple-element.24.refs_0_), channel_id=1, source_target_pairs={{0,2},{2,4},{4,6},{6,8},{8,10},{10,12},{12,14},{14,0},{1,3},{3,5},... | collective-permute-start | bytes 1081352 | tf_op jit(solution)/shard_map/ppermute | solution.py:350
  5.6 3.9 %collective-permute-done.8.b_ref = bf16[128,1152]{1,0:T(8,128)(2,1)S(1)} collective-permute-done((bf16[128,1152]{1,0:T(8,128)(2,1)S(1)}, bf16[128,1152]{1,0:T(8,128)(2,1)S(1)}, u32[]{:S(2)}, u32[]{:S(2)}) %collective-permute-start.8) | collective-permute-done | bytes 294944 | tf_op jit(solution)/shard_map/ppermute | solution.py:354
  9.6 0.0 copy-start
  9.6 2.8 %collective-permute-start.9 = (bf16[2,128,1152]{2,1,0:T(8,128)(2,1)S(1)}, bf16[2,128,1152]{2,1,0:T(8,128)(2,1)S(1)}, u32[]{:S(2)}, u32[]{:S(2)}) collective-permute-start(bf16[2,128,1152]{2,1,0:T(8,128)(2,1)S(1)} %shard_map.106.refs_1_.refs_3_), channel_id=1, source_target_pairs={{0,2},{2,4},{4,6},{6,8},{8,10},{10,12},{12,14},{14,0},{1,3},{3,5},... | collective-permute-start | bytes 1769480 | tf_op jit(solution)/shard_map/ppermute | solution.py:350
  12.4 4.0 %collective-permute-start.13 = (bf16[2,128,1152]{2,1,0:T(8,128)(2,1)S(1)}, bf16[2,128,1152]{2,1,0:T(8,128)(2,1)}, u32[]{:S(2)}, u32[]{:S(2)}) collective-permute-start(bf16[2,128,1152]{2,1,0:T(8,128)(2,1)S(1)} %shard_map.106.refs_1_.refs_3_), channel_id=1, source_target_pairs={{0,14},{2,0},{4,2},{6,4},{8,6},{10,8},{12,10},{14,12},{1,15},{3,1}... | collective-permute-start | bytes 1769480 | tf_op jit(solution)/shard_map/ppermute | solution.py:350
  16.4 1.4 %collective-permute-start.4 = (bf16[128,1408]{1,0:T(8,128)(2,1)S(1)}, bf16[128,1408]{1,0:T(8,128)(2,1)S(1)}, u32[]{:S(2)}, u32[]{:S(2)}) collective-permute-start(bf16[128,1408]{1,0:T(8,128)(2,1)S(1)} %get-tuple-element.24.refs_0_), channel_id=1, source_target_pairs={{0,14},{2,0},{4,2},{6,4},{8,6},{10,8},{12,10},{14,12},{1,15},{3,1}... | collective-permute-start | bytes 1081352 | tf_op jit(solution)/shard_map/ppermute | solution.py:350
  17.8 1.3 %collective-permute-start.20 = (bf16[128,1408]{1,0:T(8,128)(2,1)S(1)}, bf16[128,1408]{1,0:T(8,128)(2,1)S(1)}, u32[]{:S(2)}, u32[]{:S(2)}) collective-permute-start(bf16[128,1408]{1,0:T(8,128)(2,1)S(1)} %get-tuple-element.24.refs_0_), channel_id=1, source_target_pairs={{0,1},{1,0},{2,3},{3,2},{4,5},{5,4},{6,7},{7,6},{8,9},{9,8},{10,11... | collective-permute-start | bytes 1081352 | tf_op jit(solution)/shard_map/ppermute | solution.py:354
  19.1 0.0 collective-permute-done.a_ref
  19.1 0.1 collective-permute-start.1
  19.1 16.1 %collective-permute-done.4.b_ref = bf16[128,1408]{1,0:T(8,128)(2,1)S(1)} collective-permute-done((bf16[128,1408]{1,0:T(8,128)(2,1)S(1)}, bf16[128,1408]{1,0:T(8,128)(2,1)S(1)}, u32[]{:S(2)}, u32[]{:S(2)}) %collective-permute-start.4) | collective-permute-done | bytes 360480 | tf_op jit(solution)/shard_map/ppermute | solution.py:350
  35.3 3.4 %collective-permute-start.5 = (bf16[128,1408]{1,0:T(8,128)(2,1)S(1)}, bf16[128,1408]{1,0:T(8,128)(2,1)}, u32[]{:S(2)}, u32[]{:S(2)}) collective-permute-start(bf16[128,1408]{1,0:T(8,128)(2,1)S(1)} %collective-permute-done.4.b_ref), channel_id=1, source_target_pairs={{0,14},{2,0},{4,2},{6,4},{8,6},{10,8},{12,10},{14,12},{1,15},{3,1}... | collective-permute-start | bytes 1081352 | tf_op jit(solution)/shard_map/ppermute | solution.py:350
  38.7 0.1 shard_map.109.refs_3_.refs_1_
  38.7 0.0 collective-permute-done.20.refs_2_
  38.8 1.4 %collective-permute-start.21 = (bf16[2,128,1408]{2,1,0:T(8,128)(2,1)S(1)}, bf16[2,128,1408]{2,1,0:T(8,128)(2,1)S(1)}, u32[]{:S(2)}, u32[]{:S(2)}) collective-permute-start(bf16[2,128,1408]{2,1,0:T(8,128)(2,1)S(1)} %shard_map.109.refs_3_.refs_1_), channel_id=1, source_target_pairs={{0,1},{1,0},{2,3},{3,2},{4,5},{5,4},{6,7},{7,6},{8,9},{9,8},{10,11... | collective-permute-start | bytes 2162696 | tf_op jit(solution)/shard_map/ppermute | solution.py:354
  40.2 0.0 collective-permute-done.13.refs_6_.refs_5_
  40.2 2.7 %collective-permute-start.14 = (bf16[2,128,1152]{2,1,0:T(8,128)(2,1)}, bf16[2,128,1152]{2,1,0:T(8,128)(2,1)}, u32[]{:S(2)}, u32[]{:S(2)}) collective-permute-start(bf16[2,128,1152]{2,1,0:T(8,128)(2,1)} %collective-permute-done.13.refs_6_.refs_5_), channel_id=1, source_target_pairs={{0,14},{2,0},{4,2},{6,4},{8,6},{10,8},{12,10},{14,12},{1,15},{3,1}... | collective-permute-start | bytes 1769480 | tf_op jit(solution)/shard_map/ppermute | solution.py:350
  42.8 1.2 collective-permute-done.5.b_ref
  44.1 3.5 %collective-permute-start.6 = (bf16[128,1408]{1,0:T(8,128)(2,1)}, bf16[128,1408]{1,0:T(8,128)(2,1)}, u32[]{:S(2)}, u32[]{:S(2)}) collective-permute-start(bf16[128,1408]{1,0:T(8,128)(2,1)} %collective-permute-done.5.b_ref), channel_id=1, source_target_pairs={{0,14},{2,0},{4,2},{6,4},{8,6},{10,8},{12,10},{14,12},{1,15},{3,1}... | collective-permute-start | bytes 1081352 | tf_op jit(solution)/shard_map/ppermute | solution.py:350
  47.6 1.1 shard_map.108.refs_0_
  48.7 12.4 %collective-permute-done.2.a_ref = bf16[128,1408]{1,0:T(8,128)(2,1)S(1)} collective-permute-done((bf16[128,1408]{1,0:T(8,128)(2,1)S(1)}, bf16[128,1408]{1,0:T(8,128)(2,1)S(1)}, u32[]{:S(2)}, u32[]{:S(2)}) %collective-permute-start.2) | collective-permute-done | bytes 360480 | tf_op jit(solution)/shard_map/ppermute | solution.py:350
  61.0 0.2 collective-permute-start.19
  61.2 0.0 collective-permute-done.10.refs_1_.refs_4_
  61.2 0.6 copy-done.9
  61.8 0.9 copy.11.sel_ref
  62.7 0.7 stack.67.idx_ref
  63.4 0.9 slice.16
  64.3 0.2 collective-permute-done.6.b_ref
  64.5 0.4 collective-permute-start.3
  65.0 3.0 %collective-permute-start.15 = (bf16[2,128,1152]{2,1,0:T(8,128)(2,1)}, bf16[2,128,1152]{2,1,0:T(8,128)(2,1)S(1)}, u32[]{:S(2)}, u32[]{:S(2)}) collective-permute-start(bf16[2,128,1152]{2,1,0:T(8,128)(2,1)} %collective-permute-done.14.refs_3_.refs_5_), channel_id=1, source_target_pairs={{0,14},{2,0},{4,2},{6,4},{8,6},{10,8},{12,10},{14,12},{1,15},{3,1}... | collective-permute-start | bytes 1769480 | tf_op jit(solution)/shard_map/ppermute | solution.py:350
  67.9 1.0 copy-done.10
  68.9 1.2 shard_map.107.refs_0_.refs_1_
  70.1 0.0 copy-start.15
  70.1 0.0 copy-start.16
  70.1 0.0 copy-start.17
  70.2 1.4 %collective-permute-start.18 = (bf16[2,128,1408]{2,1,0:T(8,128)(2,1)S(1)}, bf16[2,128,1408]{2,1,0:T(8,128)(2,1)S(1)}, u32[]{:S(2)}, u32[]{:S(2)}) collective-permute-start(bf16[2,128,1408]{2,1,0:T(8,128)(2,1)S(1)} %shard_map.107.refs_0_.refs_1_), channel_id=1, source_target_pairs={{0,1},{1,0},{2,3},{3,2},{4,5},{5,4},{6,7},{7,6},{8,9},{9,8},{10,11... | collective-permute-start | bytes 2162696 | tf_op jit(solution)/shard_map/ppermute | solution.py:354
  71.6 1.2 %shard_map.103 = (bf16[256,2048]{1,0:T(8,128)(2,1)S(1)}, bf16[2560,256]{1,0:T(8,128)(2,1)S(1)}) custom-call(s32[16]{0:T(128)S(1)} %copy-done.11, bf16[2048,256]{1,0:T(8,128)(2,1)S(1)} %copy-done.13, bf16[256,2560]{1,0:T(8,128)(2,1)S(1)} %copy-done.12), custom_call_target="tpu_custom_call" | custom-call | flops 1000000000 | tf_op jit(solution)/shard_map/pallas_call | solution.py:59
  72.8 0.9 slice.17
  73.8 0.0 copy-start.1
  73.8 0.0 copy-start.3
  73.8 0.0 copy-start.8
  73.8 4.0 %collective-permute-done.3.a_ref = bf16[128,640]{1,0:T(8,128)(2,1)S(1)} collective-permute-done((bf16[128,640]{1,0:T(8,128)(2,1)S(1)}, bf16[128,640]{1,0:T(8,128)(2,1)S(1)}, u32[]{:S(2)}, u32[]{:S(2)}) %collective-permute-start.3) | collective-permute-done | bytes 163872 | tf_op jit(solution)/shard_map/ppermute | solution.py:350
  77.8 4.1 %shard_map.117 = (f32[20,64,128]{2,1,0:T(8,128)S(1)}, f32[20,64,128]{2,1,0:T(8,128)S(1)}, f32[20,64,128]{2,1,0:T(8,128)S(1)}, f32[20,64,128]{2,1,0:T(8,128)S(1)}...) custom-call(s32[160,64]{1,0:T(8,128)S(1)} %copy.11.sel_ref, ...), custom_call_target="tpu_custom_call" | custom-call | flops 1000000000 | tf_op jit(solution)/shard_map/pallas_call | solution.py:59
  81.9 2.6 %shard_map.114.in_ref = f32[256,2560]{1,0:T(8,128)S(1)} custom-call(bf16[256,2048]{1,0:T(8,128)(2,1)S(1)} %get-tuple-element.26.xt_ref, bf16[256,2560]{1,0:T(8,128)(2,1)S(1)} %bitcast.18, bf16[128,1408]{1,0:T(8,128)(2,1)S(1)} %copy-done.5, bf16[2,128,1408]{2,1,0:T(8,128)(2,1)S(1)} %shard_map.109.refs_3_.refs_1_, bf16[128,1408]{1,0:T(8,128)(2,1)S(1)} %copy-done.7, ...), custom_call_target="tpu_custom_call" | custom-call | flops 1000000000 | tf_op jit(solution)/shard_map/pallas_call | solution.py:59
  84.5 2.4 %shard_map.110.refs_4_ = bf16[2048,256]{1,0:T(8,128)(2,1)S(1)} custom-call(s32[16]{0:T(128)S(1)} %copy-done.11, bf16[2560,256]{1,0:T(8,128)(2,1)S(1)} %get-tuple-element.23.wt_ref, bf16[128,1408]{1,0:T(8,128)(2,1)S(1)} %copy-done.5, bf16[2,128,1152]{2,1,0:T(8,128)(2,1)S(1)} %copy-done.1, bf16[128,1408]{1,0:T(8,128)(2,1)S(1)} %copy-done.7, ...), custom_call_target="tpu_custom_call" | custom-call | flops 1000000000 | tf_op jit(solution)/shard_map/pallas_call | solution.py:59
  87.0 0.6 collective-permute-start.17
  87.5 1.5 %collective-permute-start.12 = (bf16[2,128,640]{2,1,0:T(8,128)(2,1)S(1)}, bf16[2,128,640]{2,1,0:T(8,128)(2,1)S(1)}, u32[]{:S(2)}, u32[]{:S(2)}) collective-permute-start(bf16[2,128,640]{2,1,0:T(8,128)(2,1)S(1)} %slice.18), channel_id=1, source_target_pairs={{0,2},{2,4},{4,6},{6,8},{8,10},{10,12},{12,14},{14,0},{1,3},{3,5},... | collective-permute-start | bytes 983048 | tf_op jit(solution)/shard_map/ppermute | solution.py:350
  89.1 2.2 %shard_map.111.refs_4_ = bf16[2048,256]{1,0:T(8,128)(2,1)S(1)} custom-call(s32[16]{0:T(128)S(1)} %copy-done.11, bf16[2560,256]{1,0:T(8,128)(2,1)S(1)} %get-tuple-element.23.wt_ref, bf16[2,128,1408]{2,1,0:T(8,128)(2,1)S(1)} %shard_map.108.refs_0_, bf16[2,128,1152]{2,1,0:T(8,128)(2,1)} %collective-permute-done.10.refs_1_.refs_4_, ...), custom_call_target="tpu_custom_call" | custom-call | flops 1000000000 | tf_op jit(solution)/shard_map/pallas_call | solution.py:59
  91.3 1.5 %collective-permute-start.16 = (bf16[2,128,512]{2,1,0:T(8,128)(2,1)S(1)}, bf16[2,128,512]{2,1,0:T(8,128)(2,1)S(1)}, u32[]{:S(2)}, u32[]{:S(2)}) collective-permute-start(bf16[2,128,512]{2,1,0:T(8,128)(2,1)S(1)} %slice.19), channel_id=1, source_target_pairs={{0,14},{2,0},{4,2},{6,4},{8,6},{10,8},{12,10},{14,12},{1,15},{3,1}... | collective-permute-start | bytes 786440 | tf_op jit(solution)/shard_map/ppermute | solution.py:350
  92.9 3.3 %shard_map.115.in_ref = f32[256,2560]{1,0:T(8,128)S(1)} custom-call(bf16[256,2048]{1,0:T(8,128)(2,1)S(1)} %get-tuple-element.26.xt_ref, f32[256,2560]{1,0:T(8,128)S(1)} %shard_map.114.in_ref, bf16[2,128,1408]{2,1,0:T(8,128)(2,1)S(1)} %shard_map.108.refs_0_, bf16[2,128,1408]{2,1,0:T(8,128)(2,1)S(1)} %shard_map.107.refs_0_.refs_1_, ...), custom_call_target="tpu_custom_call" | custom-call | flops 1000000000 | tf_op jit(solution)/shard_map/pallas_call | solution.py:59
  96.2 0.7 shard_map.116.in_ref
  96.9 1.5 %shard_map.112.refs_4_ = bf16[2048,256]{1,0:T(8,128)(2,1)S(1)} custom-call(s32[16]{0:T(128)S(1)} %copy-done.11, bf16[2560,256]{1,0:T(8,128)(2,1)S(1)} %get-tuple-element.23.wt_ref, bf16[2,128,1408]{2,1,0:T(8,128)(2,1)S(1)} %shard_map.107.refs_0_.refs_1_, bf16[2,128,1152]{2,1,0:T(8,128)(2,1)S(1)} %collective-permute-done.11.refs_1_, ...), custom_call_target="tpu_custom_call" | custom-call | flops 1000000000 | tf_op jit(solution)/shard_map/pallas_call | solution.py:59
  98.4 1.0 shard_map.118
  99.4 1.5 %shard_map.119 = (f32[256,1408]{1,0:T(8,128)S(1)}, f32[80,128]{1,0:T(8,128)S(1)}) custom-call(bf16[256,2048]{1,0:T(8,128)(2,1)S(1)} %get-tuple-element.26.xt_ref, f32[256,2560]{1,0:T(8,128)S(1)} %shard_map.116.in_ref, f32[20,64,128]{2,1,0:T(8,128)S(1)} %get-tuple-element.27.refs_0_, f32[20,64,128]{2,1,0:T(8,128)S(1)} %get-tuple-element.28.refs_1_, ...), custom_call_target="tpu_custom_call" | custom-call | flops 1000000000 | tf_op jit(solution)/shard_map/pallas_call | solution.py:59
  100.9 2.7 %collective-permute-start.23 = (f32[80,128]{1,0:T(8,128)S(1)}, f32[80,128]{1,0:T(8,128)S(1)}, u32[]{:S(2)}, u32[]{:S(2)}) collective-permute-start(f32[80,128]{1,0:T(8,128)S(1)} %get-tuple-element.38.sent_ref), channel_id=1, source_target_pairs={{0,32},{32,0},{1,33},{33,1},{2,34},{34,2},{3,35},{35,3},{4,36},{36... | collective-permute-start | bytes 122888 | tf_op jit(solution)/shard_map/ppermute | solution.py:360
  103.6 6.3 %collective-permute-start.24 = (f32[80,128]{1,0:T(8,128)S(1)}, f32[80,128]{1,0:T(8,128)S(1)}, u32[]{:S(2)}, u32[]{:S(2)}) collective-permute-start(f32[80,128]{1,0:T(8,128)S(1)} %get-tuple-element.38.sent_ref), channel_id=1, source_target_pairs={{0,48},{16,32},{32,16},{48,0},{1,49},{17,33},{33,17},{49,1},{2,50}... | collective-permute-start | bytes 122888 | tf_op jit(solution)/shard_map/ppermute | solution.py:363
  109.9 3.5 %shard_map.120 = bf16[256,2560]{1,0:T(8,128)(2,1)} custom-call(f32[256,1152]{1,0:T(8,128)S(1)} %get-tuple-element.35.a_ref, f32[256,1408]{1,0:T(8,128)S(1)} %get-tuple-element.37.b_ref, f32[80,128]{1,0:T(8,128)S(1)} %get-tuple-element.38.sent_ref, f32[20,64,128]{2,1,0:T(8,128)S(1)} %get-tuple-element.27.refs_0_, ...), custom_call_target="tpu_custom_call" | custom-call | flops 1000000000 | tf_op jit(solution)/shard_map/pallas_call | solution.py:59
  113.5 1.3 %collective-permute-start.26 = (f32[80,128]{1,0:T(8,128)S(1)}, f32[80,128]{1,0:T(8,128)S(1)}, u32[]{:S(2)}, u32[]{:S(2)}) collective-permute-start(f32[80,128]{1,0:T(8,128)S(1)} %add_add_fusion.1), channel_id=1, source_target_pairs={{0,64},{64,128},{128,192},{192,0},{1,65},{65,129},{129,193},{193,1... | collective-permute-start | bytes 122888 | tf_op jit(solution)/shard_map/ppermute | solution.py:360
  114.7 1.5 %collective-permute-start.27 = (f32[80,128]{1,0:T(8,128)S(1)}, f32[80,128]{1,0:T(8,128)S(1)}, u32[]{:S(2)}, u32[]{:S(2)}) collective-permute-start(f32[80,128]{1,0:T(8,128)S(1)} %add_add_fusion.1), channel_id=1, source_target_pairs={{0,192},{64,0},{128,64},{192,128},{1,193},{65,1},{129,65},{193,129... | collective-permute-start | bytes 122888 | tf_op jit(solution)/shard_map/ppermute | solution.py:360
  116.2 1.5 %collective-permute-start.25 = (f32[80,128]{1,0:T(8,128)S(1)}, f32[80,128]{1,0:T(8,128)S(1)}, u32[]{:S(2)}, u32[]{:S(2)}) collective-permute-start(f32[80,128]{1,0:T(8,128)S(1)} %add_add_fusion.1), channel_id=1, source_target_pairs={{0,128},{64,192},{128,0},{192,64},{1,129},{65,193},{129,1},{193,65... | collective-permute-start | bytes 122888 | tf_op jit(solution)/shard_map/ppermute | solution.py:360
  117.7 2.1 %shard_map.113 = bf16[2048,256]{1,0:T(8,128)(2,1)} custom-call(s32[16]{0:T(128)S(1)} %copy-done.11, bf16[2560,256]{1,0:T(8,128)(2,1)S(1)} %get-tuple-element.23.wt_ref, bf16[128,1408]{1,0:T(8,128)(2,1)S(1)} %shard_map.105.refs_0_, bf16[2,128,640]{2,1,0:T(8,128)(2,1)S(1)} %collective-permute-done.12.refs_1_.refs_8_, ...), custom_call_target="tpu_custom_call" | custom-call | flops 1000000000 | tf_op jit(solution)/shard_map/pallas_call | solution.py:59
  119.8 0.8 collective-permute-done.25
  120.7 2.6 %shard_map.121 = bf16[256,2560]{1,0:T(8,128)(2,1)} custom-call(f32[80,128]{1,0:T(8,128)S(1)} %add_add_fusion.s_ref, f32[20,64,128]{2,1,0:T(8,128)S(1)} %get-tuple-element.27.refs_0_, f32[20,64,128]{2,1,0:T(8,128)S(1)} %get-tuple-element.28.refs_1_, f32[20,64,128]{2,1,0:T(8,128)S(1)} %get-tuple-element.29.refs_2_, ...), custom_call_target="tpu_custom_call" | custom-call | flops 1000000000 | tf_op jit(solution)/shard_map/pallas_call | solution.py:59
  (55 shorter events, 0.3 us)
Async XLA Ops:
  0.6 1.1 copy-start.14
  1.8 16.0 %copy-start.4 = (bf16[128,1408]{1,0:T(8,128)(2,1)}, bf16[128,1408]{1,0:T(8,128)(2,1)S(1)}, u32[]{:S(2)}) copy-start(bf16[128,1408]{1,0:T(8,128)(2,1)S(1)} %get-tuple-element.24.refs_0_) | copy-start | bytes 1081348
  1.8 7.8 %collective-permute-start.8 = (bf16[128,1152]{1,0:T(8,128)(2,1)S(1)}, bf16[128,1152]{1,0:T(8,128)(2,1)S(1)}, u32[]{:S(2)}, u32[]{:S(2)}) collective-permute-start(bf16[128,1152]{1,0:T(8,128)(2,1)S(1)} %get-tuple-element.25.a_ref), channel_id=1, source_target_pairs={{0,1},{1,0},{2,3},{3,2},{4,5},{5,4},{6,7},{7,6},{8,9},{9,8},{10,11... | collective-permute-start | bytes 884744 | tf_op jit(solution)/shard_map/ppermute | solution.py:354
  4.0 15.1 %collective-permute-start = (bf16[128,1408]{1,0:T(8,128)(2,1)S(1)}, bf16[128,1408]{1,0:T(8,128)(2,1)S(1)}, u32[]{:S(2)}, u32[]{:S(2)}) collective-permute-start(bf16[128,1408]{1,0:T(8,128)(2,1)S(1)} %get-tuple-element.24.refs_0_), channel_id=1, source_target_pairs={{0,2},{2,4},{4,6},{6,8},{8,10},{10,12},{12,14},{14,0},{1,3},{3,5},... | collective-permute-start | bytes 1081352 | tf_op jit(solution)/shard_map/ppermute | solution.py:350
  9.6 29.1 %copy-start = (bf16[2,128,1152]{2,1,0:T(8,128)(2,1)}, bf16[2,128,1152]{2,1,0:T(8,128)(2,1)S(1)}, u32[]{:S(2)}) copy-start(bf16[2,128,1152]{2,1,0:T(8,128)(2,1)S(1)} %shard_map.106.refs_1_.refs_3_) | copy-start | bytes 1769476
  9.6 30.5 %collective-permute-start.9 = (bf16[2,128,1152]{2,1,0:T(8,128)(2,1)S(1)}, bf16[2,128,1152]{2,1,0:T(8,128)(2,1)S(1)}, u32[]{:S(2)}, u32[]{:S(2)}) collective-permute-start(bf16[2,128,1152]{2,1,0:T(8,128)(2,1)S(1)} %shard_map.106.refs_1_.refs_3_), channel_id=1, source_target_pairs={{0,2},{2,4},{4,6},{6,8},{8,10},{10,12},{12,14},{14,0},{1,3},{3,5},... | collective-permute-start | bytes 1769480 | tf_op jit(solution)/shard_map/ppermute | solution.py:350
  12.4 27.8 %collective-permute-start.13 = (bf16[2,128,1152]{2,1,0:T(8,128)(2,1)S(1)}, bf16[2,128,1152]{2,1,0:T(8,128)(2,1)}, u32[]{:S(2)}, u32[]{:S(2)}) collective-permute-start(bf16[2,128,1152]{2,1,0:T(8,128)(2,1)S(1)} %shard_map.106.refs_1_.refs_3_), channel_id=1, source_target_pairs={{0,14},{2,0},{4,2},{6,4},{8,6},{10,8},{12,10},{14,12},{1,15},{3,1}... | collective-permute-start | bytes 1769480 | tf_op jit(solution)/shard_map/ppermute | solution.py:350
  16.4 18.9 %collective-permute-start.4 = (bf16[128,1408]{1,0:T(8,128)(2,1)S(1)}, bf16[128,1408]{1,0:T(8,128)(2,1)S(1)}, u32[]{:S(2)}, u32[]{:S(2)}) collective-permute-start(bf16[128,1408]{1,0:T(8,128)(2,1)S(1)} %get-tuple-element.24.refs_0_), channel_id=1, source_target_pairs={{0,14},{2,0},{4,2},{6,4},{8,6},{10,8},{12,10},{14,12},{1,15},{3,1}... | collective-permute-start | bytes 1081352 | tf_op jit(solution)/shard_map/ppermute | solution.py:350
  17.8 21.0 %collective-permute-start.20 = (bf16[128,1408]{1,0:T(8,128)(2,1)S(1)}, bf16[128,1408]{1,0:T(8,128)(2,1)S(1)}, u32[]{:S(2)}, u32[]{:S(2)}) collective-permute-start(bf16[128,1408]{1,0:T(8,128)(2,1)S(1)} %get-tuple-element.24.refs_0_), channel_id=1, source_target_pairs={{0,1},{1,0},{2,3},{3,2},{4,5},{5,4},{6,7},{7,6},{8,9},{9,8},{10,11... | collective-permute-start | bytes 1081352 | tf_op jit(solution)/shard_map/ppermute | solution.py:354
  19.1 23.8 %collective-permute-start.1 = (bf16[128,1408]{1,0:T(8,128)(2,1)S(1)}, bf16[128,1408]{1,0:T(8,128)(2,1)S(1)}, u32[]{:S(2)}, u32[]{:S(2)}) collective-permute-start(bf16[128,1408]{1,0:T(8,128)(2,1)S(1)} %collective-permute-done.a_ref), channel_id=1, source_target_pairs={{0,2},{2,4},{4,6},{6,8},{8,10},{10,12},{12,14},{14,0},{1,3},{3,5},... | collective-permute-start | bytes 1081352 | tf_op jit(solution)/shard_map/ppermute | solution.py:350
  35.3 8.8 %collective-permute-start.5 = (bf16[128,1408]{1,0:T(8,128)(2,1)S(1)}, bf16[128,1408]{1,0:T(8,128)(2,1)}, u32[]{:S(2)}, u32[]{:S(2)}) collective-permute-start(bf16[128,1408]{1,0:T(8,128)(2,1)S(1)} %collective-permute-done.4.b_ref), channel_id=1, source_target_pairs={{0,14},{2,0},{4,2},{6,4},{8,6},{10,8},{12,10},{14,12},{1,15},{3,1}... | collective-permute-start | bytes 1081352 | tf_op jit(solution)/shard_map/ppermute | solution.py:350
  38.7 9.9 %copy-start.6 = (bf16[128,1408]{1,0:T(8,128)(2,1)}, bf16[128,1408]{1,0:T(8,128)(2,1)S(1)}, u32[]{:S(2)}) copy-start(bf16[128,1408]{1,0:T(8,128)(2,1)S(1)} %collective-permute-done.20.refs_2_) | copy-start | bytes 1081348
  38.8 31.4 %collective-permute-start.21 = (bf16[2,128,1408]{2,1,0:T(8,128)(2,1)S(1)}, bf16[2,128,1408]{2,1,0:T(8,128)(2,1)S(1)}, u32[]{:S(2)}, u32[]{:S(2)}) collective-permute-start(bf16[2,128,1408]{2,1,0:T(8,128)(2,1)S(1)} %shard_map.109.refs_3_.refs_1_), channel_id=1, source_target_pairs={{0,1},{1,0},{2,3},{3,2},{4,5},{5,4},{6,7},{7,6},{8,9},{9,8},{10,11... | collective-permute-start | bytes 2162696 | tf_op jit(solution)/shard_map/ppermute | solution.py:354
  40.1 8.5 %copy-start.2 = (bf16[2,128,1152]{2,1,0:T(8,128)(2,1)}, bf16[2,128,1152]{2,1,0:T(8,128)(2,1)S(1)}, u32[]{:S(2)}) copy-start(bf16[2,128,1152]{2,1,0:T(8,128)(2,1)S(1)} %collective-permute-done.9.refs_4_) | copy-start | bytes 1769476
  40.1 21.1 %collective-permute-start.10 = (bf16[2,128,1152]{2,1,0:T(8,128)(2,1)S(1)}, bf16[2,128,1152]{2,1,0:T(8,128)(2,1)}, u32[]{:S(2)}, u32[]{:S(2)}) collective-permute-start(bf16[2,128,1152]{2,1,0:T(8,128)(2,1)S(1)} %collective-permute-done.9.refs_4_), channel_id=1, source_target_pairs={{0,2},{2,4},{4,6},{6,8},{8,10},{10,12},{12,14},{14,0},{1,3},{3,5},... | collective-permute-start | bytes 1769480 | tf_op jit(solution)/shard_map/ppermute | solution.py:350
  40.2 24.8 %collective-permute-start.14 = (bf16[2,128,1152]{2,1,0:T(8,128)(2,1)}, bf16[2,128,1152]{2,1,0:T(8,128)(2,1)}, u32[]{:S(2)}, u32[]{:S(2)}) collective-permute-start(bf16[2,128,1152]{2,1,0:T(8,128)(2,1)} %collective-permute-done.13.refs_6_.refs_5_), channel_id=1, source_target_pairs={{0,14},{2,0},{4,2},{6,4},{8,6},{10,8},{12,10},{14,12},{1,15},{3,1}... | collective-permute-start | bytes 1769480 | tf_op jit(solution)/shard_map/ppermute | solution.py:350
  42.8 18.2 %collective-permute-start.2 = (bf16[128,1408]{1,0:T(8,128)(2,1)S(1)}, bf16[128,1408]{1,0:T(8,128)(2,1)S(1)}, u32[]{:S(2)}, u32[]{:S(2)}) collective-permute-start(bf16[128,1408]{1,0:T(8,128)(2,1)S(1)} %collective-permute-done.1.a_ref), channel_id=1, source_target_pairs={{0,2},{2,4},{4,6},{6,8},{8,10},{10,12},{12,14},{14,0},{1,3},{3,5},... | collective-permute-start | bytes 1081352 | tf_op jit(solution)/shard_map/ppermute | solution.py:350
  44.1 20.5 %collective-permute-start.6 = (bf16[128,1408]{1,0:T(8,128)(2,1)}, bf16[128,1408]{1,0:T(8,128)(2,1)}, u32[]{:S(2)}, u32[]{:S(2)}) collective-permute-start(bf16[128,1408]{1,0:T(8,128)(2,1)} %collective-permute-done.5.b_ref), channel_id=1, source_target_pairs={{0,14},{2,0},{4,2},{6,4},{8,6},{10,8},{12,10},{14,12},{1,15},{3,1}... | collective-permute-start | bytes 1081352 | tf_op jit(solution)/shard_map/ppermute | solution.py:350
  61.0 0.7 copy-start.9
  61.0 28.1 %collective-permute-start.19 = (bf16[2,128,1408]{2,1,0:T(8,128)(2,1)S(1)}, bf16[2,128,1408]{2,1,0:T(8,128)(2,1)S(1)}, u32[]{:S(2)}, u32[]{:S(2)}) collective-permute-start(bf16[2,128,1408]{2,1,0:T(8,128)(2,1)S(1)} %shard_map.108.refs_0_), channel_id=1, source_target_pairs={{0,1},{1,0},{2,3},{3,2},{4,5},{5,4},{6,7},{7,6},{8,9},{9,8},{10,11... | collective-permute-start | bytes 2162696 | tf_op jit(solution)/shard_map/ppermute | solution.py:354
  61.8 25.8 %collective-permute-start.11 = (bf16[2,128,1152]{2,1,0:T(8,128)(2,1)}, bf16[2,128,1152]{2,1,0:T(8,128)(2,1)S(1)}, u32[]{:S(2)}, u32[]{:S(2)}) collective-permute-start(bf16[2,128,1152]{2,1,0:T(8,128)(2,1)} %collective-permute-done.10.refs_1_.refs_4_), channel_id=1, source_target_pairs={{0,2},{2,4},{4,6},{6,8},{8,10},{10,12},{12,14},{14,0},{1,3},{3,5},... | collective-permute-start | bytes 1769480 | tf_op jit(solution)/shard_map/ppermute | solution.py:350
  63.4 8.2 %copy-start.11 = (s32[16]{0:T(128)S(1)}, s32[16]{0:T(128)}, u32[]{:S(2)}) copy-start(s32[16]{0:T(128)} %stack.67.idx_ref) | copy-start | bytes 196
  64.5 13.2 %collective-permute-start.3 = (bf16[128,640]{1,0:T(8,128)(2,1)S(1)}, bf16[128,640]{1,0:T(8,128)(2,1)S(1)}, u32[]{:S(2)}, u32[]{:S(2)}) collective-permute-start(bf16[128,640]{1,0:T(8,128)(2,1)S(1)} %slice.16), channel_id=1, source_target_pairs={{0,2},{2,4},{4,6},{6,8},{8,10},{10,12},{12,14},{14,0},{1,3},{3,5},... | collective-permute-start | bytes 491528 | tf_op jit(solution)/shard_map/ppermute | solution.py:350
  65.0 26.3 %collective-permute-start.15 = (bf16[2,128,1152]{2,1,0:T(8,128)(2,1)}, bf16[2,128,1152]{2,1,0:T(8,128)(2,1)S(1)}, u32[]{:S(2)}, u32[]{:S(2)}) collective-permute-start(bf16[2,128,1152]{2,1,0:T(8,128)(2,1)} %collective-permute-done.14.refs_3_.refs_5_), channel_id=1, source_target_pairs={{0,14},{2,0},{4,2},{6,4},{8,6},{10,8},{12,10},{14,12},{1,15},{3,1}... | collective-permute-start | bytes 1769480 | tf_op jit(solution)/shard_map/ppermute | solution.py:350
  67.9 1.0 copy-start.10
  68.9 2.6 %copy-start.12 = (bf16[256,2560]{1,0:T(8,128)(2,1)S(1)}, bf16[256,2560]{1,0:T(8,128)(2,1)}, u32[]{:S(2)}) copy-start(bf16[256,2560]{1,0:T(8,128)(2,1)} %w_ref.1) | copy-start | bytes 3932164
  68.9 2.6 %copy-start.13 = (bf16[2048,256]{1,0:T(8,128)(2,1)S(1)}, bf16[2048,256]{1,0:T(8,128)(2,1)}, u32[]{:S(2)}) copy-start(bf16[2048,256]{1,0:T(8,128)(2,1)} %x_ref.1) | copy-start | bytes 3145732
  70.1 7.7 %copy-start.15 = (bf16[128,256]{1,0:T(8,128)(2,1)S(1)}, bf16[128,256]{1,0:T(8,128)(2,1)}, u32[]{:S(2)}) copy-start(bf16[128,256]{1,0:T(8,128)(2,1)} %constant.133.clone.g2_ref) | copy-start | bytes 196612
  70.1 7.6 %copy-start.16 = (bf16[64,192]{1,0:T(8,128)(2,1)S(1)}, bf16[64,192]{1,0:T(8,128)(2,1)}, u32[]{:S(2)}) copy-start(bf16[64,192]{1,0:T(8,128)(2,1)} %constant.131.clone.tt_ref) | copy-start | bytes 73732
  70.1 7.6 %copy-start.17 = (bf16[128,64]{1,0:T(8,128)(2,1)S(1)}, bf16[128,64]{1,0:T(8,128)(2,1)}, u32[]{:S(2)}) copy-start(bf16[128,64]{1,0:T(8,128)(2,1)} %constant.132.clone.t2_ref) | copy-start | bytes 49156
  70.2 26.7 %collective-permute-start.18 = (bf16[2,128,1408]{2,1,0:T(8,128)(2,1)S(1)}, bf16[2,128,1408]{2,1,0:T(8,128)(2,1)S(1)}, u32[]{:S(2)}, u32[]{:S(2)}) collective-permute-start(bf16[2,128,1408]{2,1,0:T(8,128)(2,1)S(1)} %shard_map.107.refs_0_.refs_1_), channel_id=1, source_target_pairs={{0,1},{1,0},{2,3},{3,2},{4,5},{5,4},{6,7},{7,6},{8,9},{9,8},{10,11... | collective-permute-start | bytes 2162696 | tf_op jit(solution)/shard_map/ppermute | solution.py:354
  73.8 8.1 %copy-start.1 = (bf16[2,128,1152]{2,1,0:T(8,128)(2,1)S(1)}, bf16[2,128,1152]{2,1,0:T(8,128)(2,1)}, u32[]{:S(2)}) copy-start(bf16[2,128,1152]{2,1,0:T(8,128)(2,1)} %copy-done) | copy-start | bytes 1769476
  73.8 8.1 %copy-start.3 = (bf16[2,128,1152]{2,1,0:T(8,128)(2,1)S(1)}, bf16[2,128,1152]{2,1,0:T(8,128)(2,1)}, u32[]{:S(2)}) copy-start(bf16[2,128,1152]{2,1,0:T(8,128)(2,1)} %copy-done.2) | copy-start | bytes 1769476
  73.8 8.1 %copy-start.5 = (bf16[128,1408]{1,0:T(8,128)(2,1)S(1)}, bf16[128,1408]{1,0:T(8,128)(2,1)}, u32[]{:S(2)}) copy-start(bf16[128,1408]{1,0:T(8,128)(2,1)} %copy-done.4) | copy-start | bytes 1081348
  73.8 8.1 %copy-start.7 = (bf16[128,1408]{1,0:T(8,128)(2,1)S(1)}, bf16[128,1408]{1,0:T(8,128)(2,1)}, u32[]{:S(2)}) copy-start(bf16[128,1408]{1,0:T(8,128)(2,1)} %copy-done.6) | copy-start | bytes 1081348
  73.8 8.1 %copy-start.8 = (bf16[1,256,2560]{2,1,0:T(8,128)(2,1)S(1)}, bf16[1,256,2560]{2,1,0:T(8,128)(2,1)}, u32[]{:S(2)}) copy-start(bf16[1,256,2560]{2,1,0:T(8,128)(2,1)} %param.11) | copy-start | bytes 3932164
  77.8 9.1 %collective-permute-start.7 = (bf16[128,768]{1,0:T(8,128)(2,1)S(1)}, bf16[128,768]{1,0:T(8,128)(2,1)S(1)}, u32[]{:S(2)}, u32[]{:S(2)}) collective-permute-start(bf16[128,768]{1,0:T(8,128)(2,1)S(1)} %slice.17), channel_id=1, source_target_pairs={{0,14},{2,0},{4,2},{6,4},{8,6},{10,8},{12,10},{14,12},{1,15},{3,1}... | collective-permute-start | bytes 589832 | tf_op jit(solution)/shard_map/ppermute | solution.py:350
  87.0 12.4 %collective-permute-start.17 = (bf16[128,1408]{1,0:T(8,128)(2,1)S(1)}, bf16[128,1408]{1,0:T(8,128)(2,1)S(1)}, u32[]{:S(2)}, u32[]{:S(2)}) collective-permute-start(bf16[128,1408]{1,0:T(8,128)(2,1)S(1)} %shard_map.105.refs_0_), channel_id=1, source_target_pairs={{0,1},{1,0},{2,3},{3,2},{4,5},{5,4},{6,7},{7,6},{8,9},{9,8},{10,11... | collective-permute-start | bytes 1081352 | tf_op jit(solution)/shard_map/ppermute | solution.py:354
  87.5 10.8 %collective-permute-start.12 = (bf16[2,128,640]{2,1,0:T(8,128)(2,1)S(1)}, bf16[2,128,640]{2,1,0:T(8,128)(2,1)S(1)}, u32[]{:S(2)}, u32[]{:S(2)}) collective-permute-start(bf16[2,128,640]{2,1,0:T(8,128)(2,1)S(1)} %slice.18), channel_id=1, source_target_pairs={{0,2},{2,4},{4,6},{6,8},{8,10},{10,12},{12,14},{14,0},{1,3},{3,5},... | collective-permute-start | bytes 983048 | tf_op jit(solution)/shard_map/ppermute | solution.py:350
  91.3 7.0 %collective-permute-start.16 = (bf16[2,128,512]{2,1,0:T(8,128)(2,1)S(1)}, bf16[2,128,512]{2,1,0:T(8,128)(2,1)S(1)}, u32[]{:S(2)}, u32[]{:S(2)}) collective-permute-start(bf16[2,128,512]{2,1,0:T(8,128)(2,1)S(1)} %slice.19), channel_id=1, source_target_pairs={{0,14},{2,0},{4,2},{6,4},{8,6},{10,8},{12,10},{14,12},{1,15},{3,1}... | collective-permute-start | bytes 786440 | tf_op jit(solution)/shard_map/ppermute | solution.py:350
  100.9 12.5 %collective-permute-start.23 = (f32[80,128]{1,0:T(8,128)S(1)}, f32[80,128]{1,0:T(8,128)S(1)}, u32[]{:S(2)}, u32[]{:S(2)}) collective-permute-start(f32[80,128]{1,0:T(8,128)S(1)} %get-tuple-element.38.sent_ref), channel_id=1, source_target_pairs={{0,32},{32,0},{1,33},{33,1},{2,34},{34,2},{3,35},{35,3},{4,36},{36... | collective-permute-start | bytes 122888 | tf_op jit(solution)/shard_map/ppermute | solution.py:360
  103.6 9.8 %collective-permute-start.24 = (f32[80,128]{1,0:T(8,128)S(1)}, f32[80,128]{1,0:T(8,128)S(1)}, u32[]{:S(2)}, u32[]{:S(2)}) collective-permute-start(f32[80,128]{1,0:T(8,128)S(1)} %get-tuple-element.38.sent_ref), channel_id=1, source_target_pairs={{0,48},{16,32},{32,16},{48,0},{1,49},{17,33},{33,17},{49,1},{2,50}... | collective-permute-start | bytes 122888 | tf_op jit(solution)/shard_map/ppermute | solution.py:363
  109.9 3.5 %collective-permute-start.22 = (f32[80,128]{1,0:T(8,128)S(1)}, f32[80,128]{1,0:T(8,128)S(1)}, u32[]{:S(2)}, u32[]{:S(2)}) collective-permute-start(f32[80,128]{1,0:T(8,128)S(1)} %get-tuple-element.38.sent_ref), channel_id=1, source_target_pairs={{0,16},{16,0},{1,17},{17,1},{2,18},{18,2},{3,19},{19,3},{4,20},{20... | collective-permute-start | bytes 122888 | tf_op jit(solution)/shard_map/ppermute | solution.py:360
  113.5 6.4 %collective-permute-start.26 = (f32[80,128]{1,0:T(8,128)S(1)}, f32[80,128]{1,0:T(8,128)S(1)}, u32[]{:S(2)}, u32[]{:S(2)}) collective-permute-start(f32[80,128]{1,0:T(8,128)S(1)} %add_add_fusion.1), channel_id=1, source_target_pairs={{0,64},{64,128},{128,192},{192,0},{1,65},{65,129},{129,193},{193,1... | collective-permute-start | bytes 122888 | tf_op jit(solution)/shard_map/ppermute | solution.py:360
  114.7 5.1 %collective-permute-start.27 = (f32[80,128]{1,0:T(8,128)S(1)}, f32[80,128]{1,0:T(8,128)S(1)}, u32[]{:S(2)}, u32[]{:S(2)}) collective-permute-start(f32[80,128]{1,0:T(8,128)S(1)} %add_add_fusion.1), channel_id=1, source_target_pairs={{0,192},{64,0},{128,64},{192,128},{1,193},{65,1},{129,65},{193,129... | collective-permute-start | bytes 122888 | tf_op jit(solution)/shard_map/ppermute | solution.py:360
  116.2 4.4 %collective-permute-start.25 = (f32[80,128]{1,0:T(8,128)S(1)}, f32[80,128]{1,0:T(8,128)S(1)}, u32[]{:S(2)}, u32[]{:S(2)}) collective-permute-start(f32[80,128]{1,0:T(8,128)S(1)} %add_add_fusion.1), channel_id=1, source_target_pairs={{0,128},{64,192},{128,0},{192,64},{1,129},{65,193},{129,1},{193,65... | collective-permute-start | bytes 122888 | tf_op jit(solution)/shard_map/ppermute | solution.py:360

commit v2 on v1

--- a/solution.py
+++ b/solution.py
@@ -15,9 +15,8 @@
 TENSOR = ("z", "yl")
 REPLICA = ("x", "yh", "core")
 
-CUT = 1152
-A4 = 640
-B4 = 640
+CUT = 1024
+B4 = 768
 OFFSETS = (0, 1, -1, 2, -2, 3, -3, 4)
 
 
@@ -61,7 +60,7 @@
         out_shape=out,
         in_specs=specs,
         out_specs=vmem(len(out)) if many else vmem(1)[0],
-        cost_estimate=pl.CostEstimate(flops=10**9, bytes_accessed=0, transcendentals=0),
+        cost_estimate=pl.CostEstimate(flops=10**10, bytes_accessed=0, transcendentals=0),
         compiler_params=pltpu.CompilerParams(vmem_limit_bytes=8 * 2**20),
     )(*ins)
 
@@ -268,10 +267,11 @@
             sent_ref[:lo // 128 * brows, :] = ins[-1][...]
 
         def one(r, cp, p, at, cols_at):
-            u = product(acc_ref[at, cp * 128 - lo:cp * 128 - lo + 128], ct[r][cp])
-            sent_ref[p:p + 1, :] = jnp.sum(u * rt[r][cp], axis=0, keepdims=True)
-
-        over_pairs(brows, lo // 128, hi // 128, one)
+            here = pl.ds(pl.multiple_of(cp * 128 - lo, 128), 128)
+            u = product(acc_ref[at, here], ct[r][cp])
+            sent_ref[pl.ds(p, 1), :] = jnp.sum(u * rt[r][cp], axis=0, keepdims=True)
+
+        over_pairs(brows, lo // 128, hi // 128, one, 4)
 
     return call(
         kernel,
@@ -295,7 +295,7 @@
                 here = pl.ds(pl.multiple_of(cp * 128 - lo, 128), 128)
                 out_ref[at, cols_at] = (acc_ref[at, here] - e).astype(jnp.bfloat16)
 
-            over_pairs(brows, lo // 128, hi // 128, one, 3)
+            over_pairs(brows, lo // 128, hi // 128, one, 4)
 
         walk(a_ref, 0, CUT)
         walk(b_ref, CUT, cols)
@@ -386,19 +386,19 @@
         for d in (1, 2, 3):
             up, dn = zp(up, 1), zp(dn, -1)
             got[d], got[-d] = up, dn
-        got[4] = zp(up[..., :cut], 1), zp(dn[..., cut:], -1)
+        if cut == "up":
+            got[4] = zp(up, 1)
+        elif cut == "down":
+            got[4] = zp(dn, -1)
+        else:
+            got[4] = zp(up[:, :cut], 1), zp(dn[:, cut:], -1)
         return got
 
-    ra = ring(stacked(a, yp(a)), A4)
+    ra = ring(a, "up"), ring(yp(a), "down")
     rb = ring(b, B4)
     own = {0: b, 4: beside(*rb[4])}
     own.update({d: stacked(rb[d], rb[-d]) for d in (1, 2, 3)})
     other = {d: yp(own[d]) for d in range(5)}
-
-    def part_a(d):
-        if d != 4:
-            return [(ra[d], None, 0, CUT)]
-        return [(ra[4][0], None, 0, A4), (ra[4][1], None, A4, CUT - A4)]
 
     def part_b(store, d):
         return store[abs(d)], (None if d in (0, 4) else int(d < 0)), CUT, cols - CUT
@@ -411,7 +411,7 @@
         for kind, *offsets in stage:
             for d in offsets:
                 if kind == "a":
-                    pieces += [(x, sub, slot(d), 2, c, n) for x, sub, c, n in part_a(d)]
+                    pieces += [(ra[dy][d], None, slot(d) + dy, 1, 0, CUT) for dy in range(2)]
                 else:
                     x, sub, c, n = part_b(own if kind == "own" else other, d)
                     pieces.append((x, sub, slot(d) + (kind == "other"), 1, c, n))
@@ -419,9 +419,9 @@
 
     acc = wgrad_first(xt, momentum[0], w_pieces([("own", 0, 1, -1), ("other", 0), ("a", 0, 1, -1)]), scale)
     acc = wgrad_more(xt, acc, w_pieces([("own", 2, -2, 3, -3), ("other", 1, -1, 2, -2), ("a", 2, -2)]), scale)
-    acc = wgrad_more(xt, acc, w_pieces([("own", 4), ("a", 3, -3)]), scale)
+    acc = wgrad_more(xt, acc, w_pieces([("own", 4), ("other", 3, -3), ("a", 3, -3)]), scale)
     acc_a, sent_a = wgrad_encode(xt, acc, w_pieces([("a", 4)]), rts, cts, scale, None)
-    acc_b, sent = wgrad_encode(xt, acc, w_pieces([("other", 3, -3, 4)]), rts, cts, scale, sent_a)
+    acc_b, sent = wgrad_encode(xt, acc, w_pieces([("other", 4)]), rts, cts, scale, sent_a)
     total = over_replicas(sent)
 
     def g_pieces(offsets):
@@ -430,7 +430,7 @@
             for dy, store in enumerate((own, other)):
                 x, sub, c, n = part_b(store, d)
                 pieces.append((x, sub, slot(d) + dy, c, n))
-                pieces += [(x, dy, slot(d) + dy, c, n) for x, sub, c, n in part_a(d)]
+                pieces.append((ra[dy][d], None, slot(d) + dy, 0, CUT))
         return pieces
 
     dacts = None

time: 124 us -> 137 us (1.10)
  waiting for transfers between devices: 38.7 us -> 57.2 us
  local copies, waits for them, and re-layouts: 6.23 us -> 2.32 us
  Pallas kernels: 31 us -> 29.1 us
    ppermute x6, waiting for transfers between devices: 3.93 us -> 34.2 us  [yp(): return lax.ppermute(x, 'yl', [(0, 1), (1, 0)])]
    ppermute x16 -> x22, waiting for transfers between devices: 33.9 us -> 22.3 us  [zp(): return lax.ppermute(x, 'z', [(i, (i + step) % n) for i in range(n)])]
    ppermute x1, starting transfers between devices: 6.28 us -> 9.1 us  [over_replicas(): b = lax.ppermute(s, ('yh', 'core'), [(i, i ^ 3) for i in range(4)])]
    ppermute x6, starting transfers between devices: 6.98 us -> 4.57 us  [yp(): return lax.ppermute(x, 'yl', [(0, 1), (1, 0)])]
    pallas_call x19 -> x18, Pallas kernels: 31 us -> 29.1 us  [call(): pl.pallas_call(kernel, out_shape=out, in_specs=specs, out_specs=vmem(len(...]
    slice x4 -> x2, local copies, waits for them, and re-layouts: 1.92 us -> 0.03 us  [ring(): got[4] = (zp(up[:, :cut], 1), zp(dn[:, cut:], -1))]
    unnamed x37 -> x15, local copies, waits for them, and re-layouts: 3.64 us -> 2.2 us
    ppermute x16 -> x22, starting transfers between devices: 26 us -> 25.8 us  [zp(): return lax.ppermute(x, 'z', [(i, (i + step) % n) for i in range(n)])]
  transfers between devices with their start and end apart: 28 -> 34, of which waited for: 7 -> 12; matrix products, arithmetic and copies ran while one was open for 3% -> 1% of each run, Pallas kernels for 22% -> 18%
where the time goes in v2:
time: 137 us; the launch traced here: 136 us
  waiting for transfers between devices  57.2 us (42%)
  starting transfers between devices  46.5 us (34%)
  Pallas kernels  29.1 us (21%)
  local copies, waits for them, and re-layouts  2.32 us (2%)
    ppermute x6, waiting for transfers between devices, yp(): return lax.ppermute(x, 'yl', [(0, 1), (1, 0)])  34.2 us
    pallas_call x18, Pallas kernels, call(): pl.pallas_call(kernel, out_shape=out, in_specs=specs, out_specs=vmem(len(...  29.1 us
    ppermute x22, starting transfers between devices, zp(): return lax.ppermute(x, 'z', [(i, (i + step) % n) for i in range(n)])  25.8 us
    ppermute x22, waiting for transfers between devices, zp(): return lax.ppermute(x, 'z', [(i, (i + step) % n) for i in range(n)])  22.3 us
    ppermute x1, starting transfers between devices, over_replicas(): b = lax.ppermute(s, ('yh', 'core'), [(i, i ^ 3) for i in range(4)])  9.1 us
    ppermute x5, starting transfers between devices, shift(): return lax.ppermute(v, axis, [(i, (i + step) % n) for i in range(n)])  7 us
    ppermute x6, starting transfers between devices, yp(): return lax.ppermute(x, 'yl', [(0, 1), (1, 0)])  4.57 us
  transfers between devices with their start and end apart: 34, of which 12 were waited for; matrix products, arithmetic and copies ran while one was open for 1% of the time, Pallas kernels for 18%

profile of v2, /device:TPU:1, one launch (start us, length us, event | category | flops | bytes accessed | tf_op | source)
XLA Modules:
  0.0 136.1 jit_solution(14055877960619684319)
XLA Ops:
  0.7 1.2 copy-done.3
  1.9 2.5 %collective-permute-start = (bf16[128,1536]{1,0:T(8,128)(2,1)S(1)}, bf16[128,1536]{1,0:T(8,128)(2,1)}, u32[]{:S(2)}, u32[]{:S(2)}) collective-permute-start(bf16[128,1536]{1,0:T(8,128)(2,1)S(1)} %get-tuple-element.24.refs_0_), channel_id=1, source_target_pairs={{0,2},{2,4},{4,6},{6,8},{8,10},{10,12},{12,14},{14,0},{1,3},{3,5},... | collective-permute-start | bytes 1179656 | tf_op jit(solution)/shard_map/ppermute | solution.py:350
  4.5 4.0 %collective-permute-start.4 = (bf16[128,1536]{1,0:T(8,128)(2,1)S(1)}, bf16[128,1536]{1,0:T(8,128)(2,1)S(1)}, u32[]{:S(2)}, u32[]{:S(2)}) collective-permute-start(bf16[128,1536]{1,0:T(8,128)(2,1)S(1)} %get-tuple-element.24.refs_0_), channel_id=1, source_target_pairs={{0,14},{2,0},{4,2},{6,4},{8,6},{10,8},{12,10},{14,12},{1,15},{3,1}... | collective-permute-start | bytes 1179656 | tf_op jit(solution)/shard_map/ppermute | solution.py:350
  8.5 1.3 collective-permute-start.13
  9.8 2.7 %collective-permute-start.22 = (bf16[128,1024]{1,0:T(8,128)(2,1)S(1)}, bf16[128,1024]{1,0:T(8,128)(2,1)}, u32[]{:S(2)}, u32[]{:S(2)}) collective-permute-start(bf16[128,1024]{1,0:T(8,128)(2,1)S(1)} %get-tuple-element.25.refs_1_.refs_3_), channel_id=1, source_target_pairs={{0,14},{2,0},{4,2},{6,4},{8,6},{10,8},{12,10},{14,12},{1,15},{3,1}... | collective-permute-start | bytes 786440 | tf_op jit(solution)/shard_map/ppermute | solution.py:350
  12.5 0.9 copy.11.sel_ref
  13.4 0.1 stack.67.idx_ref
  13.5 0.0 copy-start.4
  13.5 0.0 copy-start.5
  13.6 0.0 copy-start.6
  13.6 1.2 shard_map.103
  14.8 4.1 %shard_map.116 = (f32[20,64,128]{2,1,0:T(8,128)S(1)}, f32[20,64,128]{2,1,0:T(8,128)S(1)}, f32[20,64,128]{2,1,0:T(8,128)S(1)}, f32[20,64,128]{2,1,0:T(8,128)S(1)}...) custom-call(s32[160,64]{1,0:T(8,128)S(1)} %copy.11.sel_ref, ...), custom_call_target="tpu_custom_call" | custom-call | flops 10000000000 | tf_op jit(solution)/shard_map/pallas_call | solution.py:58
  18.9 0.0 copy-start.1
  18.9 4.0 %collective-permute-done.8.refs_5_ = bf16[128,1024]{1,0:T(8,128)(2,1)} collective-permute-done((bf16[128,1024]{1,0:T(8,128)(2,1)S(1)}, bf16[128,1024]{1,0:T(8,128)(2,1)}, u32[]{:S(2)}, u32[]{:S(2)}) %collective-permute-start.8) | collective-permute-done | bytes 262176 | tf_op jit(solution)/shard_map/ppermute | solution.py:350
  22.9 1.3 collective-permute-start.26
  24.2 0.0 collective-permute-done.13.refs_3_.refs_4_
  24.2 1.2 collective-permute-start.14
  25.4 0.3 collective-permute-start.19
  25.7 0.1 collective-permute-start.9
  25.8 2.6 %collective-permute-start.23 = (bf16[128,1024]{1,0:T(8,128)(2,1)}, bf16[128,1024]{1,0:T(8,128)(2,1)S(1)}, u32[]{:S(2)}, u32[]{:S(2)}) collective-permute-start(bf16[128,1024]{1,0:T(8,128)(2,1)} %collective-permute-done.22.refs_8_.refs_7_), channel_id=1, source_target_pairs={{0,14},{2,0},{4,2},{6,4},{8,6},{10,8},{12,10},{14,12},{1,15},{3,1}... | collective-permute-start | bytes 786440 | tf_op jit(solution)/shard_map/ppermute | solution.py:350
  28.4 1.0 shard_map.108.refs_4_.refs_1_
  29.5 2.9 %collective-permute-done.26.refs_2_ = bf16[128,1536]{1,0:T(8,128)(2,1)S(1)} collective-permute-done((bf16[128,1536]{1,0:T(8,128)(2,1)S(1)}, bf16[128,1536]{1,0:T(8,128)(2,1)S(1)}, u32[]{:S(2)}, u32[]{:S(2)}) %collective-permute-start.26) | collective-permute-done | bytes 393248 | tf_op jit(solution)/shard_map/ppermute | solution.py:354
  32.4 2.7 %collective-permute-start.5 = (bf16[128,1536]{1,0:T(8,128)(2,1)S(1)}, bf16[128,1536]{1,0:T(8,128)(2,1)S(1)}, u32[]{:S(2)}, u32[]{:S(2)}) collective-permute-start(bf16[128,1536]{1,0:T(8,128)(2,1)S(1)} %collective-permute-done.4.b_ref), channel_id=1, source_target_pairs={{0,14},{2,0},{4,2},{6,4},{8,6},{10,8},{12,10},{14,12},{1,15},{3,1}... | collective-permute-start | bytes 1179656 | tf_op jit(solution)/shard_map/ppermute | solution.py:350
  35.1 0.3 collective-permute-start.15
  35.3 2.9 %shard_map.113.in_ref = f32[256,2560]{1,0:T(8,128)S(1)} custom-call(bf16[256,2048]{1,0:T(8,128)(2,1)S(1)} %get-tuple-element.26.xt_ref, bf16[256,2560]{1,0:T(8,128)(2,1)S(1)} %bitcast.18, bf16[128,1536]{1,0:T(8,128)(2,1)S(1)} %get-tuple-element.24.refs_0_, bf16[2,128,1536]{2,1,0:T(8,128)(2,1)S(1)} %shard_map.108.refs_4_.refs_1_, ...), custom_call_target="tpu_custom_call" | custom-call | flops 10000000000 | tf_op jit(solution)/shard_map/pallas_call | solution.py:58
  38.3 8.4 %collective-permute-done.1.a_ref = bf16[128,1536]{1,0:T(8,128)(2,1)S(1)} collective-permute-done((bf16[128,1536]{1,0:T(8,128)(2,1)}, bf16[128,1536]{1,0:T(8,128)(2,1)S(1)}, u32[]{:S(2)}, u32[]{:S(2)}) %collective-permute-start.1) | collective-permute-done | bytes 393248 | tf_op jit(solution)/shard_map/ppermute | solution.py:350
  46.7 2.7 %collective-permute-start.6 = (bf16[128,1536]{1,0:T(8,128)(2,1)S(1)}, bf16[128,1536]{1,0:T(8,128)(2,1)S(1)}, u32[]{:S(2)}, u32[]{:S(2)}) collective-permute-start(bf16[128,1536]{1,0:T(8,128)(2,1)S(1)} %collective-permute-done.5.b_ref), channel_id=1, source_target_pairs={{0,14},{2,0},{4,2},{6,4},{8,6},{10,8},{12,10},{14,12},{1,15},{3,1}... | collective-permute-start | bytes 1179656 | tf_op jit(solution)/shard_map/ppermute | solution.py:350
  49.4 0.1 shard_map.107.refs_0_
  49.4 0.3 collective-permute-start.27
  49.7 0.8 collective-permute-done.15.refs_5_.refs_7_
  50.5 5.2 %collective-permute-done.2.a_ref = bf16[128,1536]{1,0:T(8,128)(2,1)S(1)} collective-permute-done((bf16[128,1536]{1,0:T(8,128)(2,1)S(1)}, bf16[128,1536]{1,0:T(8,128)(2,1)S(1)}, u32[]{:S(2)}, u32[]{:S(2)}) %collective-permute-start.2) | collective-permute-done | bytes 393248 | tf_op jit(solution)/shard_map/ppermute | solution.py:350
  55.6 3.3 %collective-permute-done.6.b_ref = bf16[128,1536]{1,0:T(8,128)(2,1)S(1)} collective-permute-done((bf16[128,1536]{1,0:T(8,128)(2,1)S(1)}, bf16[128,1536]{1,0:T(8,128)(2,1)S(1)}, u32[]{:S(2)}, u32[]{:S(2)}) %collective-permute-start.6) | collective-permute-done | bytes 393248 | tf_op jit(solution)/shard_map/ppermute | solution.py:350
  58.9 2.3 %collective-permute-start.16 = (bf16[128,1024]{1,0:T(8,128)(2,1)S(1)}, bf16[128,1024]{1,0:T(8,128)(2,1)S(1)}, u32[]{:S(2)}, u32[]{:S(2)}) collective-permute-start(bf16[128,1024]{1,0:T(8,128)(2,1)S(1)} %collective-permute-done.15.refs_5_.refs_7_), channel_id=1, source_target_pairs={{0,14},{2,0},{4,2},{6,4},{8,6},{10,8},{12,10},{14,12},{1,15},{3,1}... | collective-permute-start | bytes 786440 | tf_op jit(solution)/shard_map/ppermute | solution.py:350
  61.1 0.1 shard_map.106.refs_0_.refs_1_
  61.3 0.1 collective-permute-start.3
  61.3 3.8 %collective-permute-done.27.refs_6_.refs_2_ = bf16[2,128,1536]{2,1,0:T(8,128)(2,1)S(1)} collective-permute-done((bf16[2,128,1536]{2,1,0:T(8,128)(2,1)S(1)}, bf16[2,128,1536]{2,1,0:T(8,128)(2,1)S(1)}, u32[]{:S(2)}, u32[]{:S(2)}) %collective-permute-start.27) | collective-permute-done | bytes 786464 | tf_op jit(solution)/shard_map/ppermute | solution.py:354
  65.1 0.3 collective-permute-start.7
  65.4 2.3 %shard_map.109.refs_6_ = bf16[2048,256]{1,0:T(8,128)(2,1)S(1)} custom-call(s32[16]{0:T(128)S(1)} %stack.67.idx_ref, bf16[2560,256]{1,0:T(8,128)(2,1)S(1)} %get-tuple-element.23.wt_ref, bf16[128,1536]{1,0:T(8,128)(2,1)S(1)} %get-tuple-element.24.refs_0_, bf16[128,1024]{1,0:T(8,128)(2,1)S(1)} %get-tuple-element.25.refs_1_.refs_3_, ...), custom_call_target="tpu_custom_call" | custom-call | flops 10000000000 | tf_op jit(solution)/shard_map/pallas_call | solution.py:58
  67.7 0.1 collective-permute-start.24
  67.8 1.4 %collective-permute-start.11 = (bf16[128,1024]{1,0:T(8,128)(2,1)S(1)}, bf16[128,1024]{1,0:T(8,128)(2,1)S(1)}, u32[]{:S(2)}, u32[]{:S(2)}) collective-permute-start(bf16[128,1024]{1,0:T(8,128)(2,1)S(1)} %collective-permute-done.10.refs_1_.refs_2_), channel_id=1, source_target_pairs={{0,2},{2,4},{4,6},{6,8},{8,10},{10,12},{12,14},{14,0},{1,3},{3,5},... | collective-permute-start | bytes 786440 | tf_op jit(solution)/shard_map/ppermute | solution.py:350
  69.3 1.2 collective-permute-start.21
  70.5 0.6 collective-permute-done.3.a_ref
  71.1 0.2 collective-permute-start.25
  71.2 1.4 %collective-permute-start.17 = (bf16[128,1024]{1,0:T(8,128)(2,1)S(1)}, bf16[128,1024]{1,0:T(8,128)(2,1)S(1)}, u32[]{:S(2)}, u32[]{:S(2)}) collective-permute-start(bf16[128,1024]{1,0:T(8,128)(2,1)S(1)} %collective-permute-done.16.refs_5_), channel_id=1, source_target_pairs={{0,14},{2,0},{4,2},{6,4},{8,6},{10,8},{12,10},{14,12},{1,15},{3,1}... | collective-permute-start | bytes 786440 | tf_op jit(solution)/shard_map/ppermute | solution.py:350
  72.7 11.0 %collective-permute-done.25.refs_2_.refs_3_ = bf16[2,128,1536]{2,1,0:T(8,128)(2,1)S(1)} collective-permute-done((bf16[2,128,1536]{2,1,0:T(8,128)(2,1)S(1)}, bf16[2,128,1536]{2,1,0:T(8,128)(2,1)S(1)}, u32[]{:S(2)}, u32[]{:S(2)}) %collective-permute-start.25) | collective-permute-done | bytes 786464 | tf_op jit(solution)/shard_map/ppermute | solution.py:354
  83.7 0.2 collective-permute-start.18
  83.9 1.4 %shard_map.110.refs_6_ = bf16[2048,256]{1,0:T(8,128)(2,1)S(1)} custom-call(s32[16]{0:T(128)S(1)} %stack.67.idx_ref, bf16[2560,256]{1,0:T(8,128)(2,1)S(1)} %get-tuple-element.23.wt_ref, bf16[2,128,1536]{2,1,0:T(8,128)(2,1)S(1)} %shard_map.107.refs_0_, bf16[128,1024]{1,0:T(8,128)(2,1)S(1)} %collective-permute-done.9.refs_1_.refs_4_, ...), custom_call_target="tpu_custom_call" | custom-call | flops 10000000000 | tf_op jit(solution)/shard_map/pallas_call | solution.py:58
  85.3 2.3 %shard_map.114.in_ref = f32[256,2560]{1,0:T(8,128)S(1)} custom-call(bf16[256,2048]{1,0:T(8,128)(2,1)S(1)} %get-tuple-element.26.xt_ref, f32[256,2560]{1,0:T(8,128)S(1)} %shard_map.113.in_ref, bf16[2,128,1536]{2,1,0:T(8,128)(2,1)S(1)} %shard_map.107.refs_0_, bf16[2,128,1536]{2,1,0:T(8,128)(2,1)S(1)} %shard_map.106.refs_0_.refs_1_, ...), custom_call_target="tpu_custom_call" | custom-call | flops 10000000000 | tf_op jit(solution)/shard_map/pallas_call | solution.py:58
  87.6 1.4 %collective-permute-start.12 = (bf16[128,1536]{1,0:T(8,128)(2,1)S(1)}, bf16[128,1536]{1,0:T(8,128)(2,1)S(1)}, u32[]{:S(2)}, u32[]{:S(2)}) collective-permute-start(bf16[128,1536]{1,0:T(8,128)(2,1)S(1)} %shard_map.105.refs_0_), channel_id=1, source_target_pairs={{0,1},{1,0},{2,3},{3,2},{4,5},{5,4},{6,7},{7,6},{8,9},{9,8},{10,11... | collective-permute-start | bytes 1179656 | tf_op jit(solution)/shard_map/ppermute | solution.py:354
  89.0 10.7 %collective-permute-done.18.refs_2_.refs_1_ = bf16[2,128,1536]{2,1,0:T(8,128)(2,1)S(1)} collective-permute-done((bf16[2,128,1536]{2,1,0:T(8,128)(2,1)S(1)}, bf16[2,128,1536]{2,1,0:T(8,128)(2,1)S(1)}, u32[]{:S(2)}, u32[]{:S(2)}) %collective-permute-start.18) | collective-permute-done | bytes 786464 | tf_op jit(solution)/shard_map/ppermute | solution.py:354
  99.7 1.3 shard_map.115.in_ref
  101.1 1.3 shard_map.117
  102.4 5.8 %collective-permute-done.12.refs_2_.refs_8_ = bf16[128,1536]{1,0:T(8,128)(2,1)S(1)} collective-permute-done((bf16[128,1536]{1,0:T(8,128)(2,1)S(1)}, bf16[128,1536]{1,0:T(8,128)(2,1)S(1)}, u32[]{:S(2)}, u32[]{:S(2)}) %collective-permute-start.12) | collective-permute-done | bytes 393248 | tf_op jit(solution)/shard_map/ppermute | solution.py:354
  108.1 1.7 %shard_map.118 = (f32[256,1536]{1,0:T(8,128)S(1)}, f32[80,128]{1,0:T(8,128)S(1)}) custom-call(bf16[256,2048]{1,0:T(8,128)(2,1)S(1)} %get-tuple-element.26.xt_ref, f32[256,2560]{1,0:T(8,128)S(1)} %shard_map.115.in_ref, f32[20,64,128]{2,1,0:T(8,128)S(1)} %get-tuple-element.27.refs_0_, f32[20,64,128]{2,1,0:T(8,128)S(1)} %get-tuple-element.28.refs_1_, ...), custom_call_target="tpu_custom_call" | custom-call | flops 10000000000 | tf_op jit(solution)/shard_map/pallas_call | solution.py:58
  109.8 2.7 %collective-permute-start.29 = (f32[80,128]{1,0:T(8,128)S(1)}, f32[80,128]{1,0:T(8,128)S(1)}, u32[]{:S(2)}, u32[]{:S(2)}) collective-permute-start(f32[80,128]{1,0:T(8,128)S(1)} %get-tuple-element.38.sent_ref), channel_id=1, source_target_pairs={{0,32},{32,0},{1,33},{33,1},{2,34},{34,2},{3,35},{35,3},{4,36},{36... | collective-permute-start | bytes 122888 | tf_op jit(solution)/shard_map/ppermute | solution.py:360
  112.5 9.1 %collective-permute-start.30 = (f32[80,128]{1,0:T(8,128)S(1)}, f32[80,128]{1,0:T(8,128)S(1)}, u32[]{:S(2)}, u32[]{:S(2)}) collective-permute-start(f32[80,128]{1,0:T(8,128)S(1)} %get-tuple-element.38.sent_ref), channel_id=1, source_target_pairs={{0,48},{16,32},{32,16},{48,0},{1,49},{17,33},{33,17},{49,1},{2,50}... | collective-permute-start | bytes 122888 | tf_op jit(solution)/shard_map/ppermute | solution.py:363
  121.6 3.2 %shard_map.119 = bf16[256,2560]{1,0:T(8,128)(2,1)} custom-call(f32[256,1024]{1,0:T(8,128)S(1)} %get-tuple-element.35.a_ref, f32[256,1536]{1,0:T(8,128)S(1)} %get-tuple-element.37.b_ref, f32[80,128]{1,0:T(8,128)S(1)} %get-tuple-element.38.sent_ref, f32[20,64,128]{2,1,0:T(8,128)S(1)} %get-tuple-element.27.refs_0_, ...), custom_call_target="tpu_custom_call" | custom-call | flops 10000000000 | tf_op jit(solution)/shard_map/pallas_call | solution.py:58
  124.9 1.4 %shard_map.111.refs_4_ = bf16[2048,256]{1,0:T(8,128)(2,1)S(1)} custom-call(s32[16]{0:T(128)S(1)} %stack.67.idx_ref, bf16[2560,256]{1,0:T(8,128)(2,1)S(1)} %get-tuple-element.23.wt_ref, bf16[2,128,1536]{2,1,0:T(8,128)(2,1)S(1)} %shard_map.106.refs_0_.refs_1_, bf16[128,1024]{1,0:T(8,128)(2,1)S(1)} %collective-permute-done.10.refs_1_.refs_2_, ...), custom_call_target="tpu_custom_call" | custom-call | flops 10000000000 | tf_op jit(solution)/shard_map/pallas_call | solution.py:58
  126.4 1.3 collective-permute-start.32
  127.7 1.5 %collective-permute-start.33 = (f32[80,128]{1,0:T(8,128)S(1)}, f32[80,128]{1,0:T(8,128)S(1)}, u32[]{:S(2)}, u32[]{:S(2)}) collective-permute-start(f32[80,128]{1,0:T(8,128)S(1)} %add_add_fusion.1), channel_id=1, source_target_pairs={{0,192},{64,0},{128,64},{192,128},{1,193},{65,1},{129,65},{193,129... | collective-permute-start | bytes 122888 | tf_op jit(solution)/shard_map/ppermute | solution.py:360
  129.1 1.5 %collective-permute-start.31 = (f32[80,128]{1,0:T(8,128)S(1)}, f32[80,128]{1,0:T(8,128)S(1)}, u32[]{:S(2)}, u32[]{:S(2)}) collective-permute-start(f32[80,128]{1,0:T(8,128)S(1)} %add_add_fusion.1), channel_id=1, source_target_pairs={{0,128},{64,192},{128,0},{192,64},{1,129},{65,193},{129,1},{193,65... | collective-permute-start | bytes 122888 | tf_op jit(solution)/shard_map/ppermute | solution.py:360
  130.7 2.0 %shard_map.112 = bf16[2048,256]{1,0:T(8,128)(2,1)} custom-call(s32[16]{0:T(128)S(1)} %stack.67.idx_ref, bf16[2560,256]{1,0:T(8,128)(2,1)S(1)} %get-tuple-element.23.wt_ref, bf16[128,1536]{1,0:T(8,128)(2,1)S(1)} %shard_map.105.refs_0_, bf16[128,1024]{1,0:T(8,128)(2,1)S(1)} %collective-permute-done.11.refs_1_.refs_8_, ...), custom_call_target="tpu_custom_call" | custom-call | flops 10000000000 | tf_op jit(solution)/shard_map/pallas_call | solution.py:58
  132.7 0.8 collective-permute-done.31
  133.5 2.6 %shard_map.120 = bf16[256,2560]{1,0:T(8,128)(2,1)} custom-call(f32[80,128]{1,0:T(8,128)S(1)} %add_add_fusion.s_ref, f32[20,64,128]{2,1,0:T(8,128)S(1)} %get-tuple-element.27.refs_0_, f32[20,64,128]{2,1,0:T(8,128)S(1)} %get-tuple-element.28.refs_1_, f32[20,64,128]{2,1,0:T(8,128)S(1)} %get-tuple-element.29.refs_2_, ...), custom_call_target="tpu_custom_call" | custom-call | flops 10000000000 | tf_op jit(solution)/shard_map/pallas_call | solution.py:58
  (42 shorter events, 0.2 us)
Async XLA Ops:
  0.6 12.9 %copy-start.2 = (bf16[2048,256]{1,0:T(8,128)(2,1)S(1)}, bf16[2048,256]{1,0:T(8,128)(2,1)}, u32[]{:S(2)}) copy-start(bf16[2048,256]{1,0:T(8,128)(2,1)} %x_ref.1) | copy-start | bytes 3145732
  0.6 12.9 %copy-start = (bf16[256,2560]{1,0:T(8,128)(2,1)S(1)}, bf16[256,2560]{1,0:T(8,128)(2,1)}, u32[]{:S(2)}) copy-start(bf16[256,2560]{1,0:T(8,128)(2,1)} %w_ref.1) | copy-start | bytes 3932164
  0.7 1.2 copy-start.3
  1.9 23.8 %collective-permute-start = (bf16[128,1536]{1,0:T(8,128)(2,1)S(1)}, bf16[128,1536]{1,0:T(8,128)(2,1)}, u32[]{:S(2)}, u32[]{:S(2)}) collective-permute-start(bf16[128,1536]{1,0:T(8,128)(2,1)S(1)} %get-tuple-element.24.refs_0_), channel_id=1, source_target_pairs={{0,2},{2,4},{4,6},{6,8},{8,10},{10,12},{12,14},{14,0},{1,3},{3,5},... | collective-permute-start | bytes 1179656 | tf_op jit(solution)/shard_map/ppermute | solution.py:350
  4.5 21.3 %collective-permute-start.4 = (bf16[128,1536]{1,0:T(8,128)(2,1)S(1)}, bf16[128,1536]{1,0:T(8,128)(2,1)S(1)}, u32[]{:S(2)}, u32[]{:S(2)}) collective-permute-start(bf16[128,1536]{1,0:T(8,128)(2,1)S(1)} %get-tuple-element.24.refs_0_), channel_id=1, source_target_pairs={{0,14},{2,0},{4,2},{6,4},{8,6},{10,8},{12,10},{14,12},{1,15},{3,1}... | collective-permute-start | bytes 1179656 | tf_op jit(solution)/shard_map/ppermute | solution.py:350
  8.5 14.5 %collective-permute-start.8 = (bf16[128,1024]{1,0:T(8,128)(2,1)S(1)}, bf16[128,1024]{1,0:T(8,128)(2,1)}, u32[]{:S(2)}, u32[]{:S(2)}) collective-permute-start(bf16[128,1024]{1,0:T(8,128)(2,1)S(1)} %get-tuple-element.25.refs_1_.refs_3_), channel_id=1, source_target_pairs={{0,2},{2,4},{4,6},{6,8},{8,10},{10,12},{12,14},{14,0},{1,3},{3,5},... | collective-permute-start | bytes 786440 | tf_op jit(solution)/shard_map/ppermute | solution.py:350
  8.5 15.7 %collective-permute-start.13 = (bf16[128,1024]{1,0:T(8,128)(2,1)S(1)}, bf16[128,1024]{1,0:T(8,128)(2,1)}, u32[]{:S(2)}, u32[]{:S(2)}) collective-permute-start(bf16[128,1024]{1,0:T(8,128)(2,1)S(1)} %get-tuple-element.25.refs_1_.refs_3_), channel_id=1, source_target_pairs={{0,1},{1,0},{2,3},{3,2},{4,5},{5,4},{6,7},{7,6},{8,9},{9,8},{10,11... | collective-permute-start | bytes 786440 | tf_op jit(solution)/shard_map/ppermute | solution.py:354
  9.8 15.6 %collective-permute-start.22 = (bf16[128,1024]{1,0:T(8,128)(2,1)S(1)}, bf16[128,1024]{1,0:T(8,128)(2,1)}, u32[]{:S(2)}, u32[]{:S(2)}) collective-permute-start(bf16[128,1024]{1,0:T(8,128)(2,1)S(1)} %get-tuple-element.25.refs_1_.refs_3_), channel_id=1, source_target_pairs={{0,14},{2,0},{4,2},{6,4},{8,6},{10,8},{12,10},{14,12},{1,15},{3,1}... | collective-permute-start | bytes 786440 | tf_op jit(solution)/shard_map/ppermute | solution.py:350
  13.5 1.3 copy-start.4
  13.5 1.3 copy-start.5
  13.6 1.3 copy-start.6
  18.9 16.4 %copy-start.1 = (bf16[1,256,2560]{2,1,0:T(8,128)(2,1)S(1)}, bf16[1,256,2560]{2,1,0:T(8,128)(2,1)}, u32[]{:S(2)}) copy-start(bf16[1,256,2560]{2,1,0:T(8,128)(2,1)} %param.11) | copy-start | bytes 3932164
  22.9 9.4 %collective-permute-start.26 = (bf16[128,1536]{1,0:T(8,128)(2,1)S(1)}, bf16[128,1536]{1,0:T(8,128)(2,1)S(1)}, u32[]{:S(2)}, u32[]{:S(2)}) collective-permute-start(bf16[128,1536]{1,0:T(8,128)(2,1)S(1)} %get-tuple-element.24.refs_0_), channel_id=1, source_target_pairs={{0,1},{1,0},{2,3},{3,2},{4,5},{5,4},{6,7},{7,6},{8,9},{9,8},{10,11... | collective-permute-start | bytes 1179656 | tf_op jit(solution)/shard_map/ppermute | solution.py:354
  24.2 8.1 %collective-permute-start.14 = (bf16[128,1024]{1,0:T(8,128)(2,1)}, bf16[128,1024]{1,0:T(8,128)(2,1)S(1)}, u32[]{:S(2)}, u32[]{:S(2)}) collective-permute-start(bf16[128,1024]{1,0:T(8,128)(2,1)} %collective-permute-done.13.refs_3_.refs_4_), channel_id=1, source_target_pairs={{0,14},{2,0},{4,2},{6,4},{8,6},{10,8},{12,10},{14,12},{1,15},{3,1}... | collective-permute-start | bytes 786440 | tf_op jit(solution)/shard_map/ppermute | solution.py:350
  25.4 9.6 %collective-permute-start.19 = (bf16[128,1024]{1,0:T(8,128)(2,1)}, bf16[128,1024]{1,0:T(8,128)(2,1)S(1)}, u32[]{:S(2)}, u32[]{:S(2)}) collective-permute-start(bf16[128,1024]{1,0:T(8,128)(2,1)} %collective-permute-done.13.refs_3_.refs_4_), channel_id=1, source_target_pairs={{0,2},{2,4},{4,6},{6,8},{8,10},{10,12},{12,14},{14,0},{1,3},{3,5},... | collective-permute-start | bytes 786440 | tf_op jit(solution)/shard_map/ppermute | solution.py:350
  25.7 23.7 %collective-permute-start.9 = (bf16[128,1024]{1,0:T(8,128)(2,1)}, bf16[128,1024]{1,0:T(8,128)(2,1)S(1)}, u32[]{:S(2)}, u32[]{:S(2)}) collective-permute-start(bf16[128,1024]{1,0:T(8,128)(2,1)} %collective-permute-done.8.refs_5_), channel_id=1, source_target_pairs={{0,2},{2,4},{4,6},{6,8},{8,10},{10,12},{12,14},{14,0},{1,3},{3,5},... | collective-permute-start | bytes 786440 | tf_op jit(solution)/shard_map/ppermute | solution.py:350
  25.8 35.4 %collective-permute-start.23 = (bf16[128,1024]{1,0:T(8,128)(2,1)}, bf16[128,1024]{1,0:T(8,128)(2,1)S(1)}, u32[]{:S(2)}, u32[]{:S(2)}) collective-permute-start(bf16[128,1024]{1,0:T(8,128)(2,1)} %collective-permute-done.22.refs_8_.refs_7_), channel_id=1, source_target_pairs={{0,14},{2,0},{4,2},{6,4},{8,6},{10,8},{12,10},{14,12},{1,15},{3,1}... | collective-permute-start | bytes 786440 | tf_op jit(solution)/shard_map/ppermute | solution.py:350
  32.4 14.3 %collective-permute-start.1 = (bf16[128,1536]{1,0:T(8,128)(2,1)}, bf16[128,1536]{1,0:T(8,128)(2,1)S(1)}, u32[]{:S(2)}, u32[]{:S(2)}) collective-permute-start(bf16[128,1536]{1,0:T(8,128)(2,1)} %collective-permute-done.a_ref), channel_id=1, source_target_pairs={{0,2},{2,4},{4,6},{6,8},{8,10},{10,12},{12,14},{14,0},{1,3},{3,5},... | collective-permute-start | bytes 1179656 | tf_op jit(solution)/shard_map/ppermute | solution.py:350
  32.4 14.3 %collective-permute-start.5 = (bf16[128,1536]{1,0:T(8,128)(2,1)S(1)}, bf16[128,1536]{1,0:T(8,128)(2,1)S(1)}, u32[]{:S(2)}, u32[]{:S(2)}) collective-permute-start(bf16[128,1536]{1,0:T(8,128)(2,1)S(1)} %collective-permute-done.4.b_ref), channel_id=1, source_target_pairs={{0,14},{2,0},{4,2},{6,4},{8,6},{10,8},{12,10},{14,12},{1,15},{3,1}... | collective-permute-start | bytes 1179656 | tf_op jit(solution)/shard_map/ppermute | solution.py:350
  35.1 15.4 %collective-permute-start.15 = (bf16[128,1024]{1,0:T(8,128)(2,1)S(1)}, bf16[128,1024]{1,0:T(8,128)(2,1)S(1)}, u32[]{:S(2)}, u32[]{:S(2)}) collective-permute-start(bf16[128,1024]{1,0:T(8,128)(2,1)S(1)} %collective-permute-done.14.refs_9_.refs_8_), channel_id=1, source_target_pairs={{0,14},{2,0},{4,2},{6,4},{8,6},{10,8},{12,10},{14,12},{1,15},{3,1}... | collective-permute-start | bytes 786440 | tf_op jit(solution)/shard_map/ppermute | solution.py:350
  46.7 8.9 %collective-permute-start.2 = (bf16[128,1536]{1,0:T(8,128)(2,1)S(1)}, bf16[128,1536]{1,0:T(8,128)(2,1)S(1)}, u32[]{:S(2)}, u32[]{:S(2)}) collective-permute-start(bf16[128,1536]{1,0:T(8,128)(2,1)S(1)} %collective-permute-done.1.a_ref), channel_id=1, source_target_pairs={{0,2},{2,4},{4,6},{6,8},{8,10},{10,12},{12,14},{14,0},{1,3},{3,5},... | collective-permute-start | bytes 1179656 | tf_op jit(solution)/shard_map/ppermute | solution.py:350
  46.7 12.2 %collective-permute-start.6 = (bf16[128,1536]{1,0:T(8,128)(2,1)S(1)}, bf16[128,1536]{1,0:T(8,128)(2,1)S(1)}, u32[]{:S(2)}, u32[]{:S(2)}) collective-permute-start(bf16[128,1536]{1,0:T(8,128)(2,1)S(1)} %collective-permute-done.5.b_ref), channel_id=1, source_target_pairs={{0,14},{2,0},{4,2},{6,4},{8,6},{10,8},{12,10},{14,12},{1,15},{3,1}... | collective-permute-start | bytes 1179656 | tf_op jit(solution)/shard_map/ppermute | solution.py:350
  49.4 15.7 %collective-permute-start.27 = (bf16[2,128,1536]{2,1,0:T(8,128)(2,1)S(1)}, bf16[2,128,1536]{2,1,0:T(8,128)(2,1)S(1)}, u32[]{:S(2)}, u32[]{:S(2)}) collective-permute-start(bf16[2,128,1536]{2,1,0:T(8,128)(2,1)S(1)} %shard_map.108.refs_4_.refs_1_), channel_id=1, source_target_pairs={{0,1},{1,0},{2,3},{3,2},{4,5},{5,4},{6,7},{7,6},{8,9},{9,8},{10,11... | collective-permute-start | bytes 2359304 | tf_op jit(solution)/shard_map/ppermute | solution.py:354
  50.5 17.4 %collective-permute-start.20 = (bf16[128,1024]{1,0:T(8,128)(2,1)S(1)}, bf16[128,1024]{1,0:T(8,128)(2,1)S(1)}, u32[]{:S(2)}, u32[]{:S(2)}) collective-permute-start(bf16[128,1024]{1,0:T(8,128)(2,1)S(1)} %collective-permute-done.19.refs_7_.refs_6_), channel_id=1, source_target_pairs={{0,2},{2,4},{4,6},{6,8},{8,10},{10,12},{12,14},{14,0},{1,3},{3,5},... | collective-permute-start | bytes 786440 | tf_op jit(solution)/shard_map/ppermute | solution.py:350
  55.6 12.1 %collective-permute-start.10 = (bf16[128,1024]{1,0:T(8,128)(2,1)S(1)}, bf16[128,1024]{1,0:T(8,128)(2,1)S(1)}, u32[]{:S(2)}, u32[]{:S(2)}) collective-permute-start(bf16[128,1024]{1,0:T(8,128)(2,1)S(1)} %collective-permute-done.9.refs_1_.refs_4_), channel_id=1, source_target_pairs={{0,2},{2,4},{4,6},{6,8},{8,10},{10,12},{12,14},{14,0},{1,3},{3,5},... | collective-permute-start | bytes 786440 | tf_op jit(solution)/shard_map/ppermute | solution.py:350
  58.9 10.4 %collective-permute-start.16 = (bf16[128,1024]{1,0:T(8,128)(2,1)S(1)}, bf16[128,1024]{1,0:T(8,128)(2,1)S(1)}, u32[]{:S(2)}, u32[]{:S(2)}) collective-permute-start(bf16[128,1024]{1,0:T(8,128)(2,1)S(1)} %collective-permute-done.15.refs_5_.refs_7_), channel_id=1, source_target_pairs={{0,14},{2,0},{4,2},{6,4},{8,6},{10,8},{12,10},{14,12},{1,15},{3,1}... | collective-permute-start | bytes 786440 | tf_op jit(solution)/shard_map/ppermute | solution.py:350
  61.3 9.8 %collective-permute-start.3 = (bf16[128,768]{1,0:T(8,128)(2,1)S(1)}, bf16[128,768]{1,0:T(8,128)(2,1)S(1)}, u32[]{:S(2)}, u32[]{:S(2)}) collective-permute-start(bf16[128,768]{1,0:T(8,128)(2,1)S(1)} %slice.8), channel_id=1, source_target_pairs={{0,2},{2,4},{4,6},{6,8},{8,10},{10,12},{12,14},{14,0},{1,3},{3,5},... | collective-permute-start | bytes 589832 | tf_op jit(solution)/shard_map/ppermute | solution.py:350
  65.1 6.1 %collective-permute-start.7 = (bf16[128,768]{1,0:T(8,128)(2,1)S(1)}, bf16[128,768]{1,0:T(8,128)(2,1)S(1)}, u32[]{:S(2)}, u32[]{:S(2)}) collective-permute-start(bf16[128,768]{1,0:T(8,128)(2,1)S(1)} %slice.9), channel_id=1, source_target_pairs={{0,14},{2,0},{4,2},{6,4},{8,6},{10,8},{12,10},{14,12},{1,15},{3,1}... | collective-permute-start | bytes 589832 | tf_op jit(solution)/shard_map/ppermute | solution.py:350
  67.7 19.9 %collective-permute-start.24 = (bf16[128,1024]{1,0:T(8,128)(2,1)S(1)}, bf16[128,1024]{1,0:T(8,128)(2,1)S(1)}, u32[]{:S(2)}, u32[]{:S(2)}) collective-permute-start(bf16[128,1024]{1,0:T(8,128)(2,1)S(1)} %collective-permute-done.23.refs_4_.refs_6_), channel_id=1, source_target_pairs={{0,14},{2,0},{4,2},{6,4},{8,6},{10,8},{12,10},{14,12},{1,15},{3,1}... | collective-permute-start | bytes 786440 | tf_op jit(solution)/shard_map/ppermute | solution.py:350
  67.8 33.2 %collective-permute-start.11 = (bf16[128,1024]{1,0:T(8,128)(2,1)S(1)}, bf16[128,1024]{1,0:T(8,128)(2,1)S(1)}, u32[]{:S(2)}, u32[]{:S(2)}) collective-permute-start(bf16[128,1024]{1,0:T(8,128)(2,1)S(1)} %collective-permute-done.10.refs_1_.refs_2_), channel_id=1, source_target_pairs={{0,2},{2,4},{4,6},{6,8},{8,10},{10,12},{12,14},{14,0},{1,3},{3,5},... | collective-permute-start | bytes 786440 | tf_op jit(solution)/shard_map/ppermute | solution.py:350
  69.3 19.7 %collective-permute-start.21 = (bf16[128,1024]{1,0:T(8,128)(2,1)S(1)}, bf16[128,1024]{1,0:T(8,128)(2,1)S(1)}, u32[]{:S(2)}, u32[]{:S(2)}) collective-permute-start(bf16[128,1024]{1,0:T(8,128)(2,1)S(1)} %collective-permute-done.20.refs_3_.refs_5_), channel_id=1, source_target_pairs={{0,2},{2,4},{4,6},{6,8},{8,10},{10,12},{12,14},{14,0},{1,3},{3,5},... | collective-permute-start | bytes 786440 | tf_op jit(solution)/shard_map/ppermute | solution.py:350
  71.1 12.7 %collective-permute-start.25 = (bf16[2,128,1536]{2,1,0:T(8,128)(2,1)S(1)}, bf16[2,128,1536]{2,1,0:T(8,128)(2,1)S(1)}, u32[]{:S(2)}, u32[]{:S(2)}) collective-permute-start(bf16[2,128,1536]{2,1,0:T(8,128)(2,1)S(1)} %shard_map.107.refs_0_), channel_id=1, source_target_pairs={{0,1},{1,0},{2,3},{3,2},{4,5},{5,4},{6,7},{7,6},{8,9},{9,8},{10,11... | collective-permute-start | bytes 2359304 | tf_op jit(solution)/shard_map/ppermute | solution.py:354
  71.2 29.8 %collective-permute-start.17 = (bf16[128,1024]{1,0:T(8,128)(2,1)S(1)}, bf16[128,1024]{1,0:T(8,128)(2,1)S(1)}, u32[]{:S(2)}, u32[]{:S(2)}) collective-permute-start(bf16[128,1024]{1,0:T(8,128)(2,1)S(1)} %collective-permute-done.16.refs_5_), channel_id=1, source_target_pairs={{0,14},{2,0},{4,2},{6,4},{8,6},{10,8},{12,10},{14,12},{1,15},{3,1}... | collective-permute-start | bytes 786440 | tf_op jit(solution)/shard_map/ppermute | solution.py:350
  83.7 16.0 %collective-permute-start.18 = (bf16[2,128,1536]{2,1,0:T(8,128)(2,1)S(1)}, bf16[2,128,1536]{2,1,0:T(8,128)(2,1)S(1)}, u32[]{:S(2)}, u32[]{:S(2)}) collective-permute-start(bf16[2,128,1536]{2,1,0:T(8,128)(2,1)S(1)} %shard_map.106.refs_0_.refs_1_), channel_id=1, source_target_pairs={{0,1},{1,0},{2,3},{3,2},{4,5},{5,4},{6,7},{7,6},{8,9},{9,8},{10,11... | collective-permute-start | bytes 2359304 | tf_op jit(solution)/shard_map/ppermute | solution.py:354
  87.6 20.5 %collective-permute-start.12 = (bf16[128,1536]{1,0:T(8,128)(2,1)S(1)}, bf16[128,1536]{1,0:T(8,128)(2,1)S(1)}, u32[]{:S(2)}, u32[]{:S(2)}) collective-permute-start(bf16[128,1536]{1,0:T(8,128)(2,1)S(1)} %shard_map.105.refs_0_), channel_id=1, source_target_pairs={{0,1},{1,0},{2,3},{3,2},{4,5},{5,4},{6,7},{7,6},{8,9},{9,8},{10,11... | collective-permute-start | bytes 1179656 | tf_op jit(solution)/shard_map/ppermute | solution.py:354
  109.8 16.5 %collective-permute-start.29 = (f32[80,128]{1,0:T(8,128)S(1)}, f32[80,128]{1,0:T(8,128)S(1)}, u32[]{:S(2)}, u32[]{:S(2)}) collective-permute-start(f32[80,128]{1,0:T(8,128)S(1)} %get-tuple-element.38.sent_ref), channel_id=1, source_target_pairs={{0,32},{32,0},{1,33},{33,1},{2,34},{34,2},{3,35},{35,3},{4,36},{36... | collective-permute-start | bytes 122888 | tf_op jit(solution)/shard_map/ppermute | solution.py:360
  112.5 13.8 %collective-permute-start.30 = (f32[80,128]{1,0:T(8,128)S(1)}, f32[80,128]{1,0:T(8,128)S(1)}, u32[]{:S(2)}, u32[]{:S(2)}) collective-permute-start(f32[80,128]{1,0:T(8,128)S(1)} %get-tuple-element.38.sent_ref), channel_id=1, source_target_pairs={{0,48},{16,32},{32,16},{48,0},{1,49},{17,33},{33,17},{49,1},{2,50}... | collective-permute-start | bytes 122888 | tf_op jit(solution)/shard_map/ppermute | solution.py:363
  121.6 4.7 %collective-permute-start.28 = (f32[80,128]{1,0:T(8,128)S(1)}, f32[80,128]{1,0:T(8,128)S(1)}, u32[]{:S(2)}, u32[]{:S(2)}) collective-permute-start(f32[80,128]{1,0:T(8,128)S(1)} %get-tuple-element.38.sent_ref), channel_id=1, source_target_pairs={{0,16},{16,0},{1,17},{17,1},{2,18},{18,2},{3,19},{19,3},{4,20},{20... | collective-permute-start | bytes 122888 | tf_op jit(solution)/shard_map/ppermute | solution.py:360
  126.4 6.3 %collective-permute-start.32 = (f32[80,128]{1,0:T(8,128)S(1)}, f32[80,128]{1,0:T(8,128)S(1)}, u32[]{:S(2)}, u32[]{:S(2)}) collective-permute-start(f32[80,128]{1,0:T(8,128)S(1)} %add_add_fusion.1), channel_id=1, source_target_pairs={{0,64},{64,128},{128,192},{192,0},{1,65},{65,129},{129,193},{193,1... | collective-permute-start | bytes 122888 | tf_op jit(solution)/shard_map/ppermute | solution.py:360
  127.7 5.0 %collective-permute-start.33 = (f32[80,128]{1,0:T(8,128)S(1)}, f32[80,128]{1,0:T(8,128)S(1)}, u32[]{:S(2)}, u32[]{:S(2)}) collective-permute-start(f32[80,128]{1,0:T(8,128)S(1)} %add_add_fusion.1), channel_id=1, source_target_pairs={{0,192},{64,0},{128,64},{192,128},{1,193},{65,1},{129,65},{193,129... | collective-permute-start | bytes 122888 | tf_op jit(solution)/shard_map/ppermute | solution.py:360
  129.1 4.4 %collective-permute-start.31 = (f32[80,128]{1,0:T(8,128)S(1)}, f32[80,128]{1,0:T(8,128)S(1)}, u32[]{:S(2)}, u32[]{:S(2)}) collective-permute-start(f32[80,128]{1,0:T(8,128)S(1)} %add_add_fusion.1), channel_id=1, source_target_pairs={{0,128},{64,192},{128,0},{192,64},{1,129},{65,193},{129,1},{193,65... | collective-permute-start | bytes 122888 | tf_op jit(solution)/shard_map/ppermute | solution.py:360
